TPU v7x, 256 devices: a whole 4x4x8 slice. The times are simulated.
256 devices in a mesh: team: 16 (over z, core), member: 16 (over x, y).
Axes of the slice: x: 4, y: 4, z: 8, core: 2. Of those that a mesh axis runs over, the one named last changes fastest.
Arguments:
- state_start: float32 [24, 1024, 2048], P(None, 'team', 'member'), may hold values from -6 to 6
- state_section: float32 [24, 1024, 2048], P(None, 'team', 'member'), may hold values from -6 to 6
- velocity: float32 [2, 1024, 2048], P(None, 'team', 'member'), may hold values from -3 to 3
- diffusivity: float32 [24], replicated, may hold values from 0.05 to 0.5
- flame_cells: int32 [256, 128], P(('team', 'member')), may hold values from 0 to 8191, as said below
- block_team: int32 [256, 1], replicated, may hold values from 0 to 15; in each aligned block of 16 rows (0 to 15, 16 to 31, ...) at most 2 rows name the same one
- w_in: bfloat16 [16, 16, 1600, 24], P('team', 'member'), may hold values from -1.25 to 1.25
- w_mid: bfloat16 [16, 16, 800, 1600], P('team', 'member'), may hold values from -0.15625 to 0.15625
- w_low: bfloat16 [16, 16, 400, 800], P('team', 'member'), may hold values from -0.21875 to 0.21875
- w_out: bfloat16 [16, 16, 24, 400], P('team', 'member'), may hold values from -0.3125 to 0.3125
Outputs:
- source_rates: float32 [24, 1024, 2048], P(None, 'team', 'member')
- new_state: float32 [24, 1024, 2048], P(None, 'team', 'member')
Inputs may be any that keep to these rules, and one draw needn't show every extreme that they name: `flame_cells`: the 128 entries of the rows of one device (rows d * 1 to d + 1 - 1) are distinct cells of that device's tile, given as i * 128 + j. `block_team`: in each aligned block of 16 rows (the flame blocks of one index of team) no regime appears more than 2 times.
All inputs are finite; a program needn't handle non-finite values.
Results may differ from a plain program's by a relative error of at most 0.0017.
The roundings to bfloat16 on the way count: a program that leaves them out, or rounds other values in their place, can miss the bound.
Values may be sent and summed in bfloat16 or wider, within the bound.
No kernel may reach another device: no remote copies, remote signals or barrier semaphores. Data moves between devices by JAX's collectives and lax.ppermute only.
A program may use at most 64 MiB of HBM per device.

v0:
```python
import math

import jax
import jax.numpy as jnp
from jax import lax
from jax.sharding import PartitionSpec as P

BLK_DEV = 1
CAP = 2


TIME_STEP = 0.25


def padded_2(array, sides, width):
    edges = {}
    for axis, dim in sides:
        size, length = (lax.axis_size(axis), array.shape[dim])
        up = [(i, (i + 1) % size) for i in range(size)]
        last = lax.slice_in_dim(array, length - width, length, axis=dim)
        initial = lax.slice_in_dim(array, 0, width, axis=dim)
        edges[dim] = (
            lax.ppermute(last, axis, up),
            lax.ppermute(initial, axis, [(b, a) for a, b in up]),
        )
    done = []
    for _, dim in sides:
        low, high = edges[dim]
        around = [(width, width) if d in done else (0, 0) for d in range(array.ndim)]
        array = jnp.concatenate([jnp.pad(low, around), array, jnp.pad(high, around)], axis=dim)
        done.append(dim)
    return array


def in_order(blocks, dim):
    dims = list(blocks.shape[1:])
    dims[dim] *= blocks.shape[0]
    return jnp.moveaxis(blocks, 0, dim).reshape(dims)


def copy_for_each(array, axis):
    length = lax.axis_size(axis)
    return lax.all_to_all(
        jnp.broadcast_to(array[None], (length, *array.shape)), axis, 0, 0, tiled=True
    )


def gather_directly(array, axis, dim):
    return in_order(copy_for_each(array, axis), dim)


def split_up(array, dim, length):
    before, after = (array.shape[:dim], array.shape[dim + 1 :])
    return jnp.moveaxis(array.reshape(*before, length, -1, *after), dim, 0)


def sent_and_summed(array, axis, dim):
    length = lax.axis_size(axis)
    blocks = lax.all_to_all(split_up(array, dim, length), axis, 0, 0, tiled=True)
    return jnp.sum(blocks, axis=0)


def build_slots(assigned, regimes, capacity):
    regime_ids = jnp.arange(regimes, dtype=jnp.int32)
    onehot = (assigned[:, None] == regime_ids[None, :]).astype(jnp.int32)
    ranks = jnp.sum((jnp.cumsum(onehot, axis=0) - onehot) * onehot, axis=1)
    slot_ids = jnp.arange(capacity, dtype=jnp.int32)
    row_ids = jnp.arange(assigned.shape[0], dtype=jnp.int32)
    match_regime = assigned[None, None, :] == regime_ids[:, None, None]
    match_rank = ranks[None, None, :] == slot_ids[None, :, None]
    matched = (match_regime & match_rank).astype(jnp.int32)
    slot_row = jnp.sum(matched * row_ids[None, None, :], axis=2)
    slot_valid = jnp.sum(matched, axis=2) > 0
    return (ranks, slot_row, slot_valid)


def shards(
    state_start,
    state_section,
    velocity,
    diffusivity,
    flame_cells,
    block_team,
    w_in,
    w_mid,
    w_low,
    w_out,
):
    regimes = lax.axis_size("team")
    members = lax.axis_size("member")
    fields, rows_x, rows_y = state_section.shape
    block_cells = flame_cells.shape[1]
    row_blocks = members * BLK_DEV
    slot_width = CAP * block_cells
    team_index = lax.axis_index("team")
    padded = padded_2(state_section.astype(jnp.bfloat16), (("team", 1), ("member", 2)), 1).astype(
        state_section.dtype
    )
    plus_x = padded[:, 2:, 1:-1]
    minus_x = padded[:, :-2, 1:-1]
    plus_y = padded[:, 1:-1, 2:]
    minus_y = padded[:, 1:-1, :-2]
    spread = diffusivity[:, None, None] * (
        plus_x + minus_x + plus_y + minus_y - 4.0 * state_section
    )
    advect = 0.5 * velocity[0][None] * (plus_x - minus_x) + 0.5 * velocity[1][None] * (
        plus_y - minus_y
    )
    flow = spread - advect
    assigned = lax.dynamic_slice_in_dim(block_team[:, 0], team_index * row_blocks, row_blocks)
    ranks, slot_row, slot_valid = build_slots(assigned, regimes, CAP)
    flat_section = state_section.reshape(fields, rows_x * rows_y)
    own_states = jnp.transpose(jnp.take(flat_section, flame_cells, axis=1), (1, 0, 2)).astype(
        jnp.bfloat16
    )
    row_states = gather_directly(own_states, "member", 0)
    picked = jnp.take(row_states, slot_row.reshape(-1), axis=0).reshape(
        regimes, CAP, fields, block_cells
    )
    picked = jnp.where(slot_valid[:, :, None, None], picked, jnp.zeros_like(picked))
    outgoing = jnp.transpose(picked, (0, 2, 1, 3)).reshape(regimes, fields, slot_width)
    incoming = lax.all_to_all(outgoing, "team", split_axis=0, concat_axis=0, tiled=True)
    weight_in = w_in[0, 0]
    weight_mid = w_mid[0, 0]
    weight_low = w_low[0, 0]
    weight_out = w_out[0, 0]
    group_size = math.gcd(regimes, max(1, 1024 // slot_width))
    grouped = incoming.reshape(regimes // group_size, group_size, fields, slot_width)

    def run_group(states):
        layer_one = jnp.einsum("hf,gfk->hgk", weight_in, states, preferred_element_type=jnp.float32)
        hidden_one = jax.nn.silu(layer_one).astype(jnp.bfloat16)
        layer_two = jnp.einsum(
            "ih,hgk->igk", weight_mid, hidden_one, preferred_element_type=jnp.float32
        )
        hidden_two = jax.nn.silu(layer_two).astype(jnp.bfloat16)
        layer_three = jnp.einsum(
            "ji,igk->jgk", weight_low, hidden_two, preferred_element_type=jnp.float32
        )
        hidden_three = jax.nn.silu(layer_three).astype(jnp.bfloat16)
        return jnp.einsum(
            "fj,jgk->gfk", weight_out, hidden_three, preferred_element_type=jnp.float32
        )

    produced = lax.map(run_group, grouped).reshape(regimes, fields, slot_width)
    returned = lax.all_to_all(produced, "team", split_axis=0, concat_axis=0, tiled=True)
    slot_rates = returned.reshape(regimes, fields, CAP, block_cells)
    row_terms = slot_rates[assigned, :, ranks]
    own_rates = sent_and_summed(row_terms, "member", 0)
    flat_rates = jnp.zeros((fields, rows_x * rows_y), jnp.float32)
    flat_rates = flat_rates.at[:, flame_cells].add(jnp.transpose(own_rates, (1, 0, 2)))
    source_rates = flat_rates.reshape(fields, rows_x, rows_y)
    new_state = 0.75 * state_start + 0.25 * (state_section + TIME_STEP * (flow + source_rates))
    return (source_rates, new_state)


def solution(mesh):
    placed = (
        P(None, "team", "member"),
        P(None, "team", "member"),
        P(None, "team", "member"),
        P(),
        P(("team", "member"), None),
        P(),
        P("team", "member", None, None),
        P("team", "member", None, None),
        P("team", "member", None, None),
        P("team", "member", None, None),
    )
    return jax.shard_map(
        shards,
        mesh=mesh,
        in_specs=placed,
        out_specs=(P(None, "team", "member"), P(None, "team", "member")),
        check_vma=False,
    )
```

profile of v0, /device:TPU:1, one launch (start us, length us, event | category | flops | bytes accessed | tf_op | source)
XLA Modules:
  0.0 131.7 jit_solution(11035493219261913234)
XLA Ops:
  0.6 0.0 copy-start.6
  0.6 0.0 copy-start.8
  0.7 0.0 copy-start.9
  0.7 0.7 fusion.55
  1.4 0.7 and_bitcast_fusion
  2.0 2.0 %copy.37 = bf16[24,64,128]{0,2,1:T(8,128)(2,1)S(1)} copy(f32[24,64,128]{2,1,0:T(8,128)} %param.13) | data formatting | bytes 1179648 | tf_op args[1]
  4.1 0.7 gather_fusion
  4.8 0.1 fusion.43
  4.9 0.1 copy.38
  4.9 0.7 broadcast_in_dim.68
  5.6 7.6 %all-to-all-start = ((bf16[16,1,24,128]{3,2,1,0:T(8,128)(2,1)}), bf16[16,1,24,128]{3,2,1,0:T(8,128)(2,1)S(1)}, u32[]{:S(2)}, u32[]{:S(2)}) async-start(bf16[16,1,24,128]{3,2,1,0:T(8,128)(2,1)} %broadcast_in_dim.68), calls=%async_computation | async-start | bytes 196608 | tf_op jit(solution)/shard_map/all_to_all | solution.py:43
  13.2 0.0 copy-done.6
  13.2 0.1 fusion.54
  13.3 0.1 iota_compare_fusion.3
  13.4 0.2 select_reduce_fusion
  13.6 0.2 fusion.44
  13.8 0.1 copy.39
  13.9 0.1 copy.35
  14.0 0.1 copy.36
  14.0 0.1 reshape.182
  14.2 5.7 %all-to-all-done = bf16[16,1,24,128]{3,2,1,0:T(8,128)(2,1)S(1)} async-done(((bf16[16,1,24,128]{3,2,1,0:T(8,128)(2,1)}), bf16[16,1,24,128]{3,2,1,0:T(8,128)(2,1)S(1)}, u32[]{:S(2)}, u32[]{:S(2)}) %all-to-all-start) | async-done | bytes 98336 | tf_op jit(solution)/shard_map/all_to_all | solution.py:43
  19.9 0.6 gather_fusion.1
  20.5 0.8 copy_bitcast_fusion.1
  21.3 10.5 %all-to-all-start.1 = ((bf16[16,24,256]{2,1,0:T(8,128)(2,1)}), bf16[16,24,256]{2,1,0:T(8,128)(2,1)S(1)}, u32[]{:S(2)}, u32[]{:S(2)}) async-start(bf16[16,24,256]{2,1,0:T(8,128)(2,1)} %copy_bitcast_fusion.1), calls=%async_computation.1 | async-start | bytes 393216 | tf_op jit(solution)/shard_map/all_to_all | solution.py:122
  31.8 10.2 %all-to-all-done.1 = bf16[16,24,256]{2,1,0:T(8,128)(2,1)S(1)} async-done(((bf16[16,24,256]{2,1,0:T(8,128)(2,1)}), bf16[16,24,256]{2,1,0:T(8,128)(2,1)S(1)}, u32[]{:S(2)}, u32[]{:S(2)}) %all-to-all-start.1) | async-done | bytes 196640 | tf_op jit(solution)/shard_map/all_to_all | solution.py:122
  42.0 0.0 copy-done.8
  42.0 0.0 copy-done.9
  42.0 49.8 %while.10 = (s32[]{:T(128)}, f32[4,4,24,256]{3,2,1,0:T(8,128)}, bf16[4,4,24,256]{3,2,1,0:T(8,128)(2,1)S(1)}, bf16[1600,24]{0,1:T(8,128)(2,1)S(1)}, bf16[800,1600...) while((s32[]{:T(128)}, f32[4,4,24,256]{3,2,1,0:T(8,128)}, ...), condition=%wide.region_5.6_spmd, body=%wide.region_4.5_spmd.sunk | while | flops 3389440000 | bytes 12560757 | solution.py:145
  42.0 0.0 copy-start.7
  42.0 8.0 %fusion.75 = f32[4,256,800]{1,2,0:T(8,128)} fusion(bf16[800,1600]{1,0:T(8,128)(2,1)} %get-tuple-element.139, bf16[1600,24]{0,1:T(8,128)(2,1)S(1)} %get-tuple-element.138, bf16[4,4,24,256]{3,2,1,0:T(8,128)(2,1)S(1)} %get-tuple-element.137, s32[]{:T(128)} %get-tuple-element.127), kind=kOutput, calls=%fused_computation.16.clone.1 | convolution fusion | flops 2708275200 | bytes 5965828 | tf_op jit(solution)/shard_map/while/body/eval_jaxpr/ih,hgk->igk/dot_general | solution.py:133
  50.1 4.4 %fusion.76 = f32[4,4,24,256]{3,2,1,0:T(8,128)} fusion(f32[4,4,24,256]{3,2,1,0:T(8,128)} %get-tuple-element.128, s32[]{:T(128)} %get-tuple-element.127, f32[4,256,800]{1,2,0:T(8,128)} %fusion.75, bf16[400,800]{1,0:T(8,128)(2,1)S(1)} %copy-done.7, bf16[24,400]{1,0:T(8,128)(2,1)S(1)} %get-tuple-element.141), kind=kOutput, calls=%fused_computation.26.clone.1 | convolution fusion | flops 681164800 | bytes 4034816 | tf_op jit(solution)/shard_map/while/body/eval_jaxpr/fj,jgk->gfk/dot_general | solution.py:141
  54.5 8.0 %fusion.75 = f32[4,256,800]{1,2,0:T(8,128)} fusion(bf16[800,1600]{1,0:T(8,128)(2,1)} %get-tuple-element.139, bf16[1600,24]{0,1:T(8,128)(2,1)S(1)} %get-tuple-element.138, bf16[4,4,24,256]{3,2,1,0:T(8,128)(2,1)S(1)} %get-tuple-element.137, s32[]{:T(128)} %get-tuple-element.127), kind=kOutput, calls=%fused_computation.16.clone.1 | convolution fusion | flops 2708275200 | bytes 5965828 | tf_op jit(solution)/shard_map/while/body/eval_jaxpr/ih,hgk->igk/dot_general | solution.py:133
  62.5 0.0 copy-done.7
  62.5 4.4 %fusion.76 = f32[4,4,24,256]{3,2,1,0:T(8,128)} fusion(f32[4,4,24,256]{3,2,1,0:T(8,128)} %get-tuple-element.128, s32[]{:T(128)} %get-tuple-element.127, f32[4,256,800]{1,2,0:T(8,128)} %fusion.75, bf16[400,800]{1,0:T(8,128)(2,1)S(1)} %copy-done.7, bf16[24,400]{1,0:T(8,128)(2,1)S(1)} %get-tuple-element.141), kind=kOutput, calls=%fused_computation.26.clone.1 | convolution fusion | flops 681164800 | bytes 4034816 | tf_op jit(solution)/shard_map/while/body/eval_jaxpr/fj,jgk->gfk/dot_general | solution.py:141
  66.9 8.0 %fusion.75 = f32[4,256,800]{1,2,0:T(8,128)} fusion(bf16[800,1600]{1,0:T(8,128)(2,1)} %get-tuple-element.139, bf16[1600,24]{0,1:T(8,128)(2,1)S(1)} %get-tuple-element.138, bf16[4,4,24,256]{3,2,1,0:T(8,128)(2,1)S(1)} %get-tuple-element.137, s32[]{:T(128)} %get-tuple-element.127), kind=kOutput, calls=%fused_computation.16.clone.1 | convolution fusion | flops 2708275200 | bytes 5965828 | tf_op jit(solution)/shard_map/while/body/eval_jaxpr/ih,hgk->igk/dot_general | solution.py:133
  74.9 4.4 %fusion.76 = f32[4,4,24,256]{3,2,1,0:T(8,128)} fusion(f32[4,4,24,256]{3,2,1,0:T(8,128)} %get-tuple-element.128, s32[]{:T(128)} %get-tuple-element.127, f32[4,256,800]{1,2,0:T(8,128)} %fusion.75, bf16[400,800]{1,0:T(8,128)(2,1)S(1)} %copy-done.7, bf16[24,400]{1,0:T(8,128)(2,1)S(1)} %get-tuple-element.141), kind=kOutput, calls=%fused_computation.26.clone.1 | convolution fusion | flops 681164800 | bytes 4034816 | tf_op jit(solution)/shard_map/while/body/eval_jaxpr/fj,jgk->gfk/dot_general | solution.py:141
  79.3 8.0 %fusion.75 = f32[4,256,800]{1,2,0:T(8,128)} fusion(bf16[800,1600]{1,0:T(8,128)(2,1)} %get-tuple-element.139, bf16[1600,24]{0,1:T(8,128)(2,1)S(1)} %get-tuple-element.138, bf16[4,4,24,256]{3,2,1,0:T(8,128)(2,1)S(1)} %get-tuple-element.137, s32[]{:T(128)} %get-tuple-element.127), kind=kOutput, calls=%fused_computation.16.clone.1 | convolution fusion | flops 2708275200 | bytes 5965828 | tf_op jit(solution)/shard_map/while/body/eval_jaxpr/ih,hgk->igk/dot_general | solution.py:133
  87.4 4.4 %fusion.76 = f32[4,4,24,256]{3,2,1,0:T(8,128)} fusion(f32[4,4,24,256]{3,2,1,0:T(8,128)} %get-tuple-element.128, s32[]{:T(128)} %get-tuple-element.127, f32[4,256,800]{1,2,0:T(8,128)} %fusion.75, bf16[400,800]{1,0:T(8,128)(2,1)S(1)} %copy-done.7, bf16[24,400]{1,0:T(8,128)(2,1)S(1)} %get-tuple-element.141), kind=kOutput, calls=%fused_computation.26.clone.1 | convolution fusion | flops 681164800 | bytes 4034816 | tf_op jit(solution)/shard_map/while/body/eval_jaxpr/fj,jgk->gfk/dot_general | solution.py:141
  91.8 3.6 %all-to-all-start.2 = ((f32[16,24,256]{2,1,0:T(8,128)}), f32[16,24,256]{2,1,0:T(8,128)S(1)}, u32[]{:S(2)}, u32[]{:S(2)}) async-start(f32[16,24,256]{2,1,0:T(8,128)} %bitcast.24), calls=%async_computation.2 | async-start | bytes 786432 | tf_op jit(solution)/shard_map/all_to_all | solution.py:146
  95.4 0.1 convert_element_type.36
  95.4 0.2 fusion.57
  95.7 0.3 collective-permute-start
  96.0 4.5 %collective-permute-start.3 = (bf16[24,64,1]{2,1,0:T(8,128)(2,1)S(1)}, bf16[24,64,1]{2,1,0:T(8,128)(2,1)}, u32[]{:S(2)}, u32[]{:S(2)}) collective-permute-start(bf16[24,64,1]{2,1,0:T(8,128)(2,1)S(1)} %get-tuple-element.69), channel_id=1, source_target_pairs={{1,0},{2,1},{3,2},{4,3},{5,4},{6,5},{7,6},{8,7},{9,8},{10,9},{11,1... | collective-permute-start | bytes 9224 | tf_op jit(solution)/shard_map/ppermute | solution.py:24
  100.5 1.9 %collective-permute-start.1 = (bf16[24,1,128]{2,1,0:T(2,128)(2,1)S(1)}, bf16[24,1,128]{2,1,0:T(2,128)(2,1)S(1)}, u32[]{:S(2)}, u32[]{:S(2)}) collective-permute-start(bf16[24,1,128]{2,1,0:T(2,128)(2,1)S(1)} %get-tuple-element.66), channel_id=1, source_target_pairs={{0,16},{16,32},{32,48},{48,64},{64,80},{80,96},{96,112},{112,128},... | collective-permute-start | bytes 18440 | tf_op jit(solution)/shard_map/ppermute | solution.py:23
  102.4 0.0 collective-permute-start.2
  102.4 0.1 fusion.53
  102.5 7.0 %all-to-all-done.2 = f32[16,24,256]{2,1,0:T(8,128)S(1)} async-done(((f32[16,24,256]{2,1,0:T(8,128)}), f32[16,24,256]{2,1,0:T(8,128)S(1)}, u32[]{:S(2)}, u32[]{:S(2)}) %all-to-all-start.2) | async-done | bytes 393248 | tf_op jit(solution)/shard_map/all_to_all | solution.py:146
  109.5 1.3 gather_fusion.2
  110.8 3.5 %all-to-all-start.3 = ((f32[16,1,24,128]{3,2,1,0:T(8,128)}), f32[16,1,24,128]{3,2,1,0:T(8,128)S(1)}, u32[]{:S(2)}, u32[]{:S(2)}) async-start(f32[16,1,24,128]{3,2,1,0:T(8,128)} %bitcast.28), calls=%async_computation.3 | async-start | bytes 393216 | tf_op jit(solution)/shard_map/all_to_all | solution.py:59
  114.3 0.6 multiply_bitcast_fusion.1
  115.0 0.0 collective-permute-done
  115.0 0.0 collective-permute-done.3
  115.0 0.0 collective-permute-done.1
  115.0 0.0 collective-permute-done.2
  115.0 1.8 %fusion.41 = f32[24,66,130]{2,1,0:T(8,128)S(1)} fusion(bf16[24,64,1]{2,1,0:T(8,128)(2,1)} %collective-permute-done.3, bf16[24,64,1]{2,1,0:T(8,128)(2,1)S(1)} %collective-permute-done, bf16[24,1,128]{2,1,0:T(2,128)(2,1)} %collective-permute-done.2, bf16[24,64,128]{2,1,0:T(8,128)(2,1)S(1)} %convert_element_type.36, ...), kind=kLoop, calls=%fused_computation.42 | loop fusion | flops 2882880 | bytes 1235328 | tf_op jit(solution)/shard_map/convert_element_type | solution.py:96
  116.8 5.4 %all-to-all-done.3 = f32[16,1,24,128]{3,2,1,0:T(8,128)S(1)} async-done(((f32[16,1,24,128]{3,2,1,0:T(8,128)}), f32[16,1,24,128]{3,2,1,0:T(8,128)S(1)}, u32[]{:S(2)}, u32[]{:S(2)}) %all-to-all-start.3) | async-done | bytes 196640 | tf_op jit(solution)/shard_map/all_to_all | solution.py:59
  122.2 0.1 copy.44
  122.3 3.2 %scatter_custom_fusion = f32[24,8192]{0,1:T(8,128)} fusion(s32[128]{0:T(128)S(1)} %fusion.55, f32[128,24]{1,0:T(8,128)S(1)} %copy.44, f32[]{:T(128)} %constant.36.clone.1), kind=kCustom, calls=%fused_computation.35 | custom fusion | flops 3072 | bytes 786436 | tf_op jit(solution)/shard_map/scatter-add | solution.py:151
  125.5 2.9 %copy.46 = f32[24,64,128]{2,1,0:T(8,128)S(1)} copy(f32[24,64,128]{0,2,1:T(8,128)} %bitcast.136) | data formatting | bytes 1572864
  128.5 0.0 copy-start.1
  128.5 0.0 copy-done.2
  128.5 0.0 copy-done.3
  128.5 0.0 copy-done.5
  128.5 3.2 %multiply_add_fusion = f32[24,64,128]{2,1,0:T(8,128)} fusion(f32[24,64,128]{2,1,0:T(8,128)S(1)} %copy-done, f32[24,64,128]{2,1,0:T(8,128)S(1)} %copy.46, f32[24,66,130]{2,1,0:T(8,128)S(1)} %fusion.41, f32[24,64,128]{2,1,0:T(8,128)} %param.12, f32[64,128]{1,0:T(8,128)S(1)} %copy-done.3, f32[64,128]{1,0:T(8,128)S(1)} %copy-done.2, f32[24]{0:T(128)S(1)} %copy-done.5), kind=kLoop, calls=%fused_computation.44 | loop fusion | flops 3538944 | bytes 6357088 | tf_op jit(solution)/shard_map/add | solution.py:153
  (24 shorter events, 0.2 us)
Async XLA Ops:
  0.6 12.6 %copy-start.6 = (s32[256,1]{0,1:T(1,128)S(1)}, s32[256,1]{0,1:T(1,128)}, u32[]{:S(2)}) copy-start(s32[256,1]{0,1:T(1,128)} %param.17) | copy-start | bytes 3076
  0.6 41.4 %copy-start.8 = (bf16[1,1,1600,24]{2,3,1,0:T(8,128)(2,1)S(1)}, bf16[1,1,1600,24]{2,3,1,0:T(8,128)(2,1)}, u32[]{:S(2)}) copy-start(bf16[1,1,1600,24]{2,3,1,0:T(8,128)(2,1)} %param.18) | copy-start | bytes 230404
  0.7 41.4 %copy-start.9 = (bf16[1,1,24,400]{3,2,1,0:T(8,128)(2,1)S(1)}, bf16[1,1,24,400]{3,2,1,0:T(8,128)(2,1)}, u32[]{:S(2)}) copy-start(bf16[1,1,24,400]{3,2,1,0:T(8,128)(2,1)} %param.21) | copy-start | bytes 57604
  5.6 14.3 %all-to-all-start = ((bf16[16,1,24,128]{3,2,1,0:T(8,128)(2,1)}), bf16[16,1,24,128]{3,2,1,0:T(8,128)(2,1)S(1)}, u32[]{:S(2)}, u32[]{:S(2)}) async-start(bf16[16,1,24,128]{3,2,1,0:T(8,128)(2,1)} %broadcast_in_dim.68), calls=%async_computation | async-start | bytes 196608 | tf_op jit(solution)/shard_map/all_to_all | solution.py:43
  21.3 20.7 %all-to-all-start.1 = ((bf16[16,24,256]{2,1,0:T(8,128)(2,1)}), bf16[16,24,256]{2,1,0:T(8,128)(2,1)S(1)}, u32[]{:S(2)}, u32[]{:S(2)}) async-start(bf16[16,24,256]{2,1,0:T(8,128)(2,1)} %copy_bitcast_fusion.1), calls=%async_computation.1 | async-start | bytes 393216 | tf_op jit(solution)/shard_map/all_to_all | solution.py:122
  42.0 53.4 %copy-start = (f32[24,64,128]{2,1,0:T(8,128)S(1)}, f32[24,64,128]{2,1,0:T(8,128)}, u32[]{:S(2)}) copy-start(f32[24,64,128]{2,1,0:T(8,128)} %param.13) | copy-start | bytes 2359300
  42.0 8.1 %copy-start.7 = (bf16[400,800]{1,0:T(8,128)(2,1)S(1)}, bf16[400,800]{1,0:T(8,128)(2,1)}, u32[]{:S(2)}) copy-start(bf16[400,800]{1,0:T(8,128)(2,1)} %get-tuple-element.140) | copy-start | bytes 1920004 | tf_op jit(solution)/shard_map/while
  54.5 8.0 %copy-start.7 = (bf16[400,800]{1,0:T(8,128)(2,1)S(1)}, bf16[400,800]{1,0:T(8,128)(2,1)}, u32[]{:S(2)}) copy-start(bf16[400,800]{1,0:T(8,128)(2,1)} %get-tuple-element.140) | copy-start | bytes 1920004 | tf_op jit(solution)/shard_map/while
  66.9 8.0 %copy-start.7 = (bf16[400,800]{1,0:T(8,128)(2,1)S(1)}, bf16[400,800]{1,0:T(8,128)(2,1)}, u32[]{:S(2)}) copy-start(bf16[400,800]{1,0:T(8,128)(2,1)} %get-tuple-element.140) | copy-start | bytes 1920004 | tf_op jit(solution)/shard_map/while
  79.3 8.0 %copy-start.7 = (bf16[400,800]{1,0:T(8,128)(2,1)S(1)}, bf16[400,800]{1,0:T(8,128)(2,1)}, u32[]{:S(2)}) copy-start(bf16[400,800]{1,0:T(8,128)(2,1)} %get-tuple-element.140) | copy-start | bytes 1920004 | tf_op jit(solution)/shard_map/while
  91.8 22.6 %copy-start.4 = (f32[2,64,128]{2,1,0:T(8,128)S(1)}, f32[2,64,128]{2,1,0:T(8,128)}, u32[]{:S(2)}) copy-start(f32[2,64,128]{2,1,0:T(8,128)} %param.14) | copy-start | bytes 196612
  91.8 17.7 %all-to-all-start.2 = ((f32[16,24,256]{2,1,0:T(8,128)}), f32[16,24,256]{2,1,0:T(8,128)S(1)}, u32[]{:S(2)}, u32[]{:S(2)}) async-start(f32[16,24,256]{2,1,0:T(8,128)} %bitcast.24), calls=%async_computation.2 | async-start | bytes 786432 | tf_op jit(solution)/shard_map/all_to_all | solution.py:146
  95.7 19.3 %collective-permute-start = (bf16[24,64,1]{2,1,0:T(8,128)(2,1)S(1)}, bf16[24,64,1]{2,1,0:T(8,128)(2,1)S(1)}, u32[]{:S(2)}, u32[]{:S(2)}) collective-permute-start(bf16[24,64,1]{2,1,0:T(8,128)(2,1)S(1)} %get-tuple-element.68), channel_id=1, source_target_pairs={{0,1},{1,2},{2,3},{3,4},{4,5},{5,6},{6,7},{7,8},{8,9},{9,10},{10,1... | collective-permute-start | bytes 9224 | tf_op jit(solution)/shard_map/ppermute | solution.py:23
  96.0 19.0 %collective-permute-start.3 = (bf16[24,64,1]{2,1,0:T(8,128)(2,1)S(1)}, bf16[24,64,1]{2,1,0:T(8,128)(2,1)}, u32[]{:S(2)}, u32[]{:S(2)}) collective-permute-start(bf16[24,64,1]{2,1,0:T(8,128)(2,1)S(1)} %get-tuple-element.69), channel_id=1, source_target_pairs={{1,0},{2,1},{3,2},{4,3},{5,4},{6,5},{7,6},{8,7},{9,8},{10,9},{11,1... | collective-permute-start | bytes 9224 | tf_op jit(solution)/shard_map/ppermute | solution.py:24
  100.5 14.4 %collective-permute-start.1 = (bf16[24,1,128]{2,1,0:T(2,128)(2,1)S(1)}, bf16[24,1,128]{2,1,0:T(2,128)(2,1)S(1)}, u32[]{:S(2)}, u32[]{:S(2)}) collective-permute-start(bf16[24,1,128]{2,1,0:T(2,128)(2,1)S(1)} %get-tuple-element.66), channel_id=1, source_target_pairs={{0,16},{16,32},{32,48},{48,64},{64,80},{80,96},{96,112},{112,128},... | collective-permute-start | bytes 18440 | tf_op jit(solution)/shard_map/ppermute | solution.py:23
  102.4 12.6 %collective-permute-start.2 = (bf16[24,1,128]{2,1,0:T(2,128)(2,1)S(1)}, bf16[24,1,128]{2,1,0:T(2,128)(2,1)}, u32[]{:S(2)}, u32[]{:S(2)}) collective-permute-start(bf16[24,1,128]{2,1,0:T(2,128)(2,1)S(1)} %get-tuple-element.67), channel_id=1, source_target_pairs={{16,0},{32,16},{48,32},{64,48},{80,64},{96,80},{112,96},{128,112},... | collective-permute-start | bytes 18440 | tf_op jit(solution)/shard_map/ppermute | solution.py:24
  110.8 11.4 %all-to-all-start.3 = ((f32[16,1,24,128]{3,2,1,0:T(8,128)}), f32[16,1,24,128]{3,2,1,0:T(8,128)S(1)}, u32[]{:S(2)}, u32[]{:S(2)}) async-start(f32[16,1,24,128]{3,2,1,0:T(8,128)} %bitcast.28), calls=%async_computation.3 | async-start | bytes 393216 | tf_op jit(solution)/shard_map/all_to_all | solution.py:59
  125.5 3.0 %copy-start.2 = (f32[64,128]{1,0:T(8,128)S(1)}, f32[64,128]{1,0:T(8,128)}, u32[]{:S(2)}) copy-start(f32[64,128]{1,0:T(8,128)} %get-tuple-element.70) | copy-start | bytes 98308
  125.5 3.0 %copy-start.3 = (f32[64,128]{1,0:T(8,128)S(1)}, f32[64,128]{1,0:T(8,128)}, u32[]{:S(2)}) copy-start(f32[64,128]{1,0:T(8,128)} %get-tuple-element.71) | copy-start | bytes 98308
  125.5 3.0 %copy-start.5 = (f32[24]{0:T(128)S(1)}, f32[24]{0:T(128)}, u32[]{:S(2)}) copy-start(f32[24]{0:T(128)} %param.15) | copy-start | bytes 292
  128.5 3.2 %copy-start.1 = (f32[24,64,128]{2,1,0:T(8,128)}, f32[24,64,128]{2,1,0:T(8,128)S(1)}, u32[]{:S(2)}) copy-start(f32[24,64,128]{2,1,0:T(8,128)S(1)} %copy.46) | copy-start | bytes 2359300
where the time goes:
time: 132 us
  matrix products  49.7 us (38%)
  starting transfers between devices  31.9 us (24%)
  waiting for transfers between devices  28.3 us (21%)
  other arithmetic  11.8 us (9%)
  local copies, waits for them, and re-layouts  9.16 us (7%)
    dot_general x4, matrix products, run_group(): jnp.einsum('ih,hgk->igk', weight_mid, hidden_one, preferred_element_type=...  32 us
    dot_general x4, matrix products, run_group(): jnp.einsum('fj,jgk->gfk', weight_out, hidden_three, preferred_element_typ...  17.7 us
    all_to_all x1, starting transfers between devices, shards(): lax.all_to_all(outgoing, 'team', split_axis=0, concat_axis=0, tiled=True)  10.5 us
    all_to_all x1, waiting for transfers between devices, shards(): lax.all_to_all(outgoing, 'team', split_axis=0, concat_axis=0, tiled=True)  10.2 us
    all_to_all x1, starting transfers between devices, copy_for_each(): lax.all_to_all(jnp.broadcast_to(array[None], (length, *array.shape)), axi...  7.57 us
    all_to_all x1, waiting for transfers between devices, shards(): lax.all_to_all(produced, 'team', split_axis=0, concat_axis=0, tiled=True)  7.01 us
    all_to_all x1, waiting for transfers between devices, copy_for_each(): lax.all_to_all(jnp.broadcast_to(array[None], (length, *array.shape)), axi...  5.74 us
    all_to_all x1, waiting for transfers between devices, sent_and_summed(): lax.all_to_all(split_up(array, dim, length), axis, 0, 0, tiled=True)  5.38 us
  transfers between devices with their start and end apart: 8, of which 4 were waited for; matrix products, arithmetic and copies ran while one was open for 4% of the time, Pallas kernels for 0%

commit v1 on v0

v1 whole, which is shorter than its diff:
```python
import jax
import jax.numpy as jnp
from jax import lax
from jax.experimental import pallas as pl
from jax.experimental.pallas import tpu as pltpu
from jax.sharding import Mesh, PartitionSpec as P

BF = jnp.bfloat16
F32 = jnp.float32
I32 = jnp.int32
TIME_STEP = 0.25
VM = pl.BlockSpec(memory_space=pltpu.VMEM)
SM = pl.BlockSpec(memory_space=pltpu.SMEM)
HB = pl.BlockSpec(memory_space=pl.ANY)
PARAMS = pltpu.CompilerParams(vmem_limit_bytes=56 * 2**20)

SRC, POS, OWN, SIB, N_OWN, N_SIB, CORE = 0, 32, 64, 80, 96, 97, 98


def dot(a, b, dims=((1,), (0,))):
    return lax.dot_general(a, b, (dims, ((), ())), preferred_element_type=F32)


def silu(x):
    h = 0.5 * x
    return (h * jnp.tanh(h) + h).astype(BF)


def iota(shape, dim):
    return lax.broadcasted_iota(I32, shape, dim)


def table_kernel(ids, team_ref, out):
    z, c, q = ids[0], ids[1], ids[2]
    n = team_ref.shape[1]
    across = jnp.broadcast_to(team_ref[...].astype(F32), (n, n))
    down = across.T
    row, lane = iota((n, n), 0), iota((n, n), 1)
    before = (across == down) & (lane < row)
    rank = jnp.sum(jnp.where(before, 1.0, 0.0), axis=1, keepdims=True).astype(I32)
    near = before & ((lane // 32) == (row // 32))
    local = jnp.sum(jnp.where(near, 1.0, 0.0), axis=1, keepdims=True).astype(I32)
    shape = (n, 128)
    g = down[:, :128].astype(I32)
    rank = jnp.broadcast_to(rank, shape)
    local = jnp.broadcast_to(local, shape)
    b, s = iota(shape, 0), iota(shape, 1)
    core = (rank + g) & 1
    slot = (g & 1) * 2 + (local >> 1)
    place = (g >> 1) * 4 + slot
    here = (b >> 5) == z
    mine = core == c
    own = mine & (g == 2 * z + c)
    sib = mine & (g == 2 * z + 1 - c)
    arrives = (b >> 5) * 4 + slot
    zero = jnp.zeros(shape, I32)
    value = jnp.where((s < POS) & here & mine & (place == s), b & 31, zero)
    value = jnp.where((s >= POS) & (s < OWN) & here & ((b & 31) == s - POS), place, value)
    value = jnp.where((s >= OWN) & (s < SIB) & own & ((rank >> 1) == s - OWN), arrives, value)
    value = jnp.where((s >= SIB) & (s < N_OWN) & sib & ((rank >> 1) == s - SIB), arrives, value)
    value = jnp.where((s == N_OWN) & own, 1, value)
    value = jnp.where((s == N_SIB) & sib, 1, value)
    value = jnp.where((s == CORE) & (b == (2 * z + c) * 16 + q), core, value)
    out[...] = jnp.sum(value.astype(F32), axis=0, keepdims=True).astype(I32)


def front_kernel(cells, state, blocks, x_low, x_high, y_edges):
    fields, rows, cols = state.shape
    width = cells.shape[1]
    column = cells[...] & (cols - 1)
    line = cells[...] >> (cols.bit_length() - 1)
    picks = jnp.where(iota((cols, width), 0) == column, 1.0, 0.0).astype(BF)
    flat = state[...].astype(BF).reshape(fields * rows, cols)
    found = dot(flat, picks).reshape(fields, rows, width)
    at_row = (iota((rows, width), 0) == line)[None]
    own = jnp.sum(jnp.where(at_row, found, 0.0), axis=1).astype(BF)
    for k in range(blocks.shape[0]):
        blocks[k] = own
    x_low[...] = state[:, 0, :].astype(BF)
    x_high[...] = state[:, rows - 1, :].astype(BF)
    e, j = iota((16, cols), 0), iota((16, cols), 1)
    ends = jnp.where(((e == 0) & (j == 0)) | ((e == 1) & (j == cols - 1)), 1.0, 0.0).astype(BF)
    y_edges[...] = dot(ends, flat, ((1,), (1,)))[0:2].astype(BF)


def select_kernel(base, table, rows, out):
    for k in range(out.shape[0]):
        out[k] = rows[table[0, base + k]]


def network_kernel(table, x, *refs):
    hbm, out = refs[:8], refs[8]
    scratch, sems = refs[9:13], refs[13]
    copies = [
        [pltpu.make_async_copy(hbm[4 * w + k], scratch[k].at[w], sems.at[w, k]) for k in range(4)]
        for w in range(2)
    ]
    for w in range(2):
        for copy in copies[w]:
            copy.start()
    for w, (first, count) in enumerate(((OWN, N_OWN), (SIB, N_SIB))):
        for copy in copies[w]:
            copy.wait()
        n = table[0, count]

        def step(k, _, w=w, first=first, n=n):
            at = [table[0, first + jnp.minimum(4 * k + i, n - 1)] for i in range(4)]
            states = jnp.concatenate([x[i] for i in at], axis=1)
            one = silu(dot(scratch[0][w], states, ((0,), (0,))))
            two = silu(dot(scratch[1][w], one))
            three = silu(dot(scratch[2][w], two))
            rates = dot(scratch[3][w], three)
            for i, a in enumerate(at):
                out[a] = rates[:, i * 128 : (i + 1) * 128]
            return 0

        lax.fori_loop(0, (n + 3) // 4, step, 0)


def base_kernel(diff, start, state, velocity, up, down, y_edges, out):
    fields, rows, cols = state.shape
    e, j = iota((2, cols), 0), iota((2, cols), 1)
    ends = jnp.where(((e == 0) & (j == 0)) | ((e == 1) & (j == cols - 1)), 1.0, 0.0).astype(BF)
    sides = dot(y_edges[...], ends, ((0,), (0,))).reshape(fields, rows, cols)
    row, lane = iota((rows, cols), 0), iota((rows, cols), 1)
    half_x, half_y = 0.5 * velocity[0], 0.5 * velocity[1]
    for f in range(fields):
        u = state[f]
        plus_x = jnp.where(row == rows - 1, down[f : f + 1].astype(F32), pltpu.roll(u, rows - 1, 0))
        minus_x = jnp.where(row == 0, up[f : f + 1].astype(F32), pltpu.roll(u, 1, 0))
        plus_y = jnp.where(lane == cols - 1, sides[f], pltpu.roll(u, cols - 1, 1))
        minus_y = jnp.where(lane == 0, sides[f], pltpu.roll(u, 1, 1))
        flow = diff[f] * (plus_x + minus_x + plus_y + minus_y - 4.0 * u)
        flow = flow - half_x * (plus_x - minus_x) - half_y * (plus_y - minus_y)
        out[f] = 0.75 * start[f] + 0.25 * (u + TIME_STEP * flow)


def final_kernel(table, cells, parts, base, source, new):
    fields, rows, cols = base.shape
    width = cells.shape[1]
    first = table[0, CORE] * 16
    rates = parts[first]
    for n in range(1, 16):
        rates = rates + parts[first + n]
    high = rates.astype(BF).astype(F32)
    low = rates - high
    column = cells[...] & (cols - 1)
    line = cells[...] >> (cols.bit_length() - 1)
    at_row = iota((rows, width), 0) == line
    at_col = jnp.where(iota((cols, width), 0) == column, 1.0, 0.0).astype(BF)
    at_col = jnp.concatenate([at_col, at_col], axis=1)
    for f in range(fields):
        left = jnp.where(at_row, high[f : f + 1], 0.0)
        right = jnp.where(at_row, low[f : f + 1], 0.0)
        spread = jnp.concatenate([left, right], axis=1).astype(BF)
        placed = dot(spread, at_col, ((1,), (1,)))
        source[f] = placed
        new[f] = base[f] + (0.25 * TIME_STEP) * placed


def call(body, out_shape, in_specs, out_specs=None, scratch=(), name=None):
    if out_specs is None:
        out_specs = jax.tree.map(lambda _: VM, out_shape)
    return pl.pallas_call(
        body, out_shape=out_shape, in_specs=in_specs, out_specs=out_specs,
        scratch_shapes=scratch, compiler_params=PARAMS, name=name,
    )


def shards(start, state, velocity, diffusivity, cells, block_team, w_in, w_mid, w_low, w_out):
    fields, rows, cols = state.shape
    width = cells.shape[1]
    sds = jax.ShapeDtypeStruct
    members = lax.axis_size("member")
    teams = lax.axis_size("z") * lax.axis_size("core")
    up = [(i, (i + 1) % 16) for i in range(16)]
    back = [(b, a) for a, b in up]
    swap = [(0, 1), (1, 0)]
    plane = ("core", "member")
    line = ("z", "core")

    ids = jnp.stack([lax.axis_index(a) for a in ("z", "core", "member")]).astype(I32)
    weights = [w_in[0, 0].T, w_mid[0, 0], w_low[0, 0], w_out[0, 0]]
    partner = [lax.ppermute(w, "core", swap) for w in weights]

    blocks, x_low, x_high, y_edges = call(
        front_kernel,
        (sds((2 * members, fields, width), BF), sds((fields, cols), BF), sds((fields, cols), BF),
         sds((2, fields * rows), BF)),
        [VM, VM], name="front",
    )(cells, state)
    gathered = lax.all_to_all(blocks, plane, 0, 0, tiled=True)
    table = call(table_kernel, sds((1, 128), I32), [SM, VM], name="table")(ids, block_team.T)
    outgoing = call(
        lambda *r: select_kernel(SRC, *r), sds((32, fields, width), BF), [SM, VM], name="select"
    )(table, gathered)
    incoming = lax.all_to_all(outgoing, "z", 0, 0, tiled=True)

    from_up = lax.ppermute(x_high, line, up)
    from_down = lax.ppermute(x_low, line, back)
    from_left = lax.ppermute(y_edges[1:2], "member", up)
    from_right = lax.ppermute(y_edges[0:1], "member", back)

    produced = call(
        network_kernel, sds((32, fields, width), F32), [SM, VM] + [HB] * 8,
        scratch=[pltpu.VMEM((2, *w.shape), BF) for w in weights] + [pltpu.SemaphoreType.DMA((2, 4))],
        name="networks",
    )(table, incoming, *weights, *partner)
    returned = lax.all_to_all(produced, "z", 0, 0, tiled=True)
    base = call(
        base_kernel, sds(state.shape, F32), [SM] + [VM] * 6, name="base"
    )(diffusivity, start, state, velocity, from_up, from_down,
      jnp.concatenate([from_left, from_right], axis=0))
    terms = call(
        lambda *r: select_kernel(POS, *r), sds((32, fields, width), F32), [SM, VM], name="pick"
    )(table, returned)
    parts = lax.all_to_all(terms, plane, 0, 0, tiled=True)
    return call(
        final_kernel, (sds(state.shape, F32), sds(state.shape, F32)), [SM, VM, VM, VM], name="final"
    )(table, cells, parts, base)


def solution(mesh):
    team, member = mesh.devices.shape
    own_mesh = Mesh(mesh.devices.reshape(team // 2, 2, member), ("z", "core", "member"))
    line = ("z", "core")
    tile = P(None, line, "member")
    weight = P(line, "member", None, None)
    return jax.shard_map(
        shards,
        mesh=own_mesh,
        in_specs=(tile, tile, tile, P(), P((*line, "member"), None), P(), weight, weight, weight, weight),
        out_specs=(tile, tile),
        check_vma=False,
    )
```

time: 132 us -> 105 us (0.80)
  matrix products: 49.7 us -> 0 us
  Pallas kernels: 0 us -> 29 us
  blocking collectives: 0 us -> 19.5 us
  waiting for transfers between devices: 28.3 us -> 17.3 us
  other arithmetic: 11.8 us -> 1.28 us
  local copies, waits for them, and re-layouts: 9.16 us -> 4.83 us
    dot_general x8 -> x0, matrix products: 49.7 us -> none  [the longest x4 32 us: run_group(): jnp.einsum('ih,hgk->igk', weight_mid, hidden_one, preferred_element_type=...]
    pallas_call x0 -> x7, Pallas kernels: none -> 29 us  [the longest x1 15.6 us: shards(): call(network_kernel, sds((32, fields, width), F32), [SM, VM] + [HB] * 8,...]
    all_to_all x0 -> x1, blocking collectives: none -> 19.5 us  [shards(): returned = lax.all_to_all(produced, 'z', 0, 0, tiled=True)]
    all_to_all x4 -> x3, waiting for transfers between devices: 28.3 us -> 12.7 us  [the longest x1 6.78 us: shards(): incoming = lax.all_to_all(outgoing, 'z', 0, 0, tiled=True)]
    ppermute x4 -> x8, waiting for transfers between devices: 0.01 us -> 4.57 us  [the longest x1 3.27 us: shards(): from_left = lax.ppermute(y_edges[1:2], 'member', up)]
    all_to_all x4 -> x3, starting transfers between devices: 25.2 us -> 21.6 us  [the longest x1 8.19 us: shards(): incoming = lax.all_to_all(outgoing, 'z', 0, 0, tiled=True)]
    ppermute x4 -> x8, starting transfers between devices: 6.72 us -> 10.2 us  [the longest x4 4.38 us: shards(): partner = [lax.ppermute(w, 'core', swap) for w in weights]]
    add x1 -> x0, other arithmetic: 3.2 us -> none  [shards(): 0.75 * state_start]
  transfers between devices with their start and end apart: 8 -> 11, of which waited for: 4 -> 4; matrix products, arithmetic and copies ran while one was open for 4% -> 1% of each run, Pallas kernels for 0% -> 8%
where the time goes in v1:
time: 105 us; the launch traced here: 104 us
  starting transfers between devices  31.8 us (30%)
  Pallas kernels  29 us (28%)
  blocking collectives  19.5 us (19%)
  waiting for transfers between devices  17.3 us (16%)
  local copies, waits for them, and re-layouts  4.83 us (5%)
  other arithmetic  1.28 us (1%)
    all_to_all x1, blocking collectives, shards(): returned = lax.all_to_all(produced, 'z', 0, 0, tiled=True)  19.5 us
    pallas_call x1, Pallas kernels, shards(): call(network_kernel, sds((32, fields, width), F32), [SM, VM] + [HB] * 8,...  15.6 us
    all_to_all x1, starting transfers between devices, shards(): incoming = lax.all_to_all(outgoing, 'z', 0, 0, tiled=True)  8.19 us
    all_to_all x1, starting transfers between devices, shards(): parts = lax.all_to_all(terms, plane, 0, 0, tiled=True)  7.62 us
    all_to_all x1, waiting for transfers between devices, shards(): incoming = lax.all_to_all(outgoing, 'z', 0, 0, tiled=True)  6.78 us
    all_to_all x1, waiting for transfers between devices, shards(): gathered = lax.all_to_all(blocks, plane, 0, 0, tiled=True)  5.95 us
    all_to_all x1, starting transfers between devices, shards(): gathered = lax.all_to_all(blocks, plane, 0, 0, tiled=True)  5.79 us
    unnamed x22, local copies, waits for them, and re-layouts  4.81 us
  transfers between devices with their start and end apart: 11, of which 4 were waited for; matrix products, arithmetic and copies ran while one was open for 1% of the time, Pallas kernels for 8%

profile of v1, /device:TPU:1, one launch (start us, length us, event | category | flops | bytes accessed | tf_op | source)
XLA Modules:
  0.0 104.5 jit_solution(9051367314755025373)
XLA Ops:
  0.6 3.3 %collective-permute-start.1 = (bf16[800,1600]{1,0:T(8,128)(2,1)}, bf16[800,1600]{1,0:T(8,128)(2,1)S(1)}, u32[]{:S(2)}, u32[]{:S(2)}) collective-permute-start(bf16[800,1600]{1,0:T(8,128)(2,1)} %bitcast.10), channel_id=1, source_target_pairs={{0,16},{16,0},{1,17},{17,1},{2,18},{18,2},{3,19},{19,3},{4,20},{20... | collective-permute-start | bytes 7680008 | tf_op jit(solution)/shard_map/ppermute | solution.py:184
  3.9 0.1 collective-permute-start.2
  4.0 2.2 %front.1 = (bf16[32,24,128]{2,1,0:T(8,128)(2,1)}, bf16[24,128]{1,0:T(8,128)(2,1)}, bf16[24,128]{1,0:T(8,128)(2,1)}, bf16[2,1536]{1,0:T(2,128)(2,1)}) custom-call(s32[1,128]{1,0:T(1,128)} %cells.3, f32[24,64,128]{2,1,0:T(8,128)} %state.3), custom_call_target="tpu_custom_call" | custom-call | tf_op jit(solution)/shard_map/front/pallas_call | solution.py:186
  6.2 5.8 %all-to-all-start = ((bf16[32,24,128]{2,1,0:T(8,128)(2,1)}), bf16[32,24,128]{2,1,0:T(8,128)(2,1)S(1)}, u32[]{:S(2)}, u32[]{:S(2)}) async-start(bf16[32,24,128]{2,1,0:T(8,128)(2,1)} %get-tuple-element.6), calls=%async_computation | async-start | bytes 393216 | tf_op jit(solution)/shard_map/all_to_all | solution.py:192
  12.0 0.7 pad_add_fusion.ids
  12.7 1.6 %table.1.r_0_ = s32[1,128]{1,0:T(1,128)} custom-call(s32[3]{0:T(128)} %pad_add_fusion.ids, s32[1,256]{1,0:T(1,128)} %bitcast.18), custom_call_target="tpu_custom_call" | custom-call | tf_op jit(solution)/shard_map/table/pallas_call | solution.py:193
  14.3 6.0 %all-to-all-done.r_1_ = bf16[32,24,128]{2,1,0:T(8,128)(2,1)S(1)} async-done(((bf16[32,24,128]{2,1,0:T(8,128)(2,1)}), bf16[32,24,128]{2,1,0:T(8,128)(2,1)S(1)}, u32[]{:S(2)}, u32[]{:S(2)}) %all-to-all-start) | async-done | bytes 196640 | tf_op jit(solution)/shard_map/all_to_all | solution.py:192
  20.2 0.0 copy-start.2
  20.2 0.7 copy-done.2
  20.9 1.6 %select.1 = bf16[32,24,128]{2,1,0:T(8,128)(2,1)} custom-call(s32[1,128]{1,0:T(1,128)} %table.1.r_0_, bf16[32,24,128]{2,1,0:T(8,128)(2,1)} %copy-done.2), custom_call_target="tpu_custom_call" | custom-call | tf_op jit(solution)/shard_map/select/pallas_call | solution.py:194
  22.5 8.2 %all-to-all-start.1 = ((bf16[32,24,128]{2,1,0:T(8,128)(2,1)}), bf16[32,24,128]{2,1,0:T(8,128)(2,1)S(1)}, u32[]{:S(2)}, u32[]{:S(2)}) async-start(bf16[32,24,128]{2,1,0:T(8,128)(2,1)} %select.1), calls=%async_computation.1 | async-start | bytes 393216 | tf_op jit(solution)/shard_map/all_to_all | solution.py:197
  30.7 0.9 collective-permute-start
  31.6 0.0 copy-start.6
  31.6 0.0 copy-start.10
  31.6 0.0 copy-start.9
  31.6 0.1 collective-permute-start.3
  31.7 1.3 %collective-permute-done.3.refs_7_ = bf16[24,400]{1,0:T(8,128)(2,1)S(1)} collective-permute-done((bf16[24,400]{1,0:T(8,128)(2,1)}, bf16[24,400]{1,0:T(8,128)(2,1)S(1)}, u32[]{:S(2)}, u32[]{:S(2)}) %collective-permute-start.3) | collective-permute-done | bytes 19232 | tf_op jit(solution)/shard_map/ppermute | solution.py:184
  33.0 0.0 copy-start.5
  33.0 0.0 collective-permute-done.refs_4_
  33.0 0.0 copy-start.4
  33.0 6.8 %all-to-all-done.1.x = bf16[32,24,128]{2,1,0:T(8,128)(2,1)S(1)} async-done(((bf16[32,24,128]{2,1,0:T(8,128)(2,1)}), bf16[32,24,128]{2,1,0:T(8,128)(2,1)S(1)}, u32[]{:S(2)}, u32[]{:S(2)}) %all-to-all-start.1) | async-done | bytes 196640 | tf_op jit(solution)/shard_map/all_to_all | solution.py:197
  39.8 0.0 copy-start.3
  39.8 0.0 collective-permute-done.2.refs_6_
  39.8 0.0 collective-permute-done.1.refs_5_
  39.8 0.0 copy-done.5
  39.8 0.0 copy-done.4
  39.8 0.6 copy-done.3
  40.5 0.0 copy-start
  40.5 1.5 %copy-done = bf16[800,1600]{1,0:T(8,128)(2,1)} copy-done((bf16[800,1600]{1,0:T(8,128)(2,1)}, bf16[800,1600]{1,0:T(8,128)(2,1)S(1)}, u32[]{:S(2)}) %copy-start) | copy-done | bytes 2560024
  42.0 15.6 %networks.1 = f32[32,24,128]{2,1,0:T(8,128)} custom-call(s32[1,128]{1,0:T(1,128)} %table.1.r_0_, bf16[32,24,128]{2,1,0:T(8,128)(2,1)} %copy-done.3, bf16[24,1600]{1,0:T(8,128)(2,1)} %bitcast.15, bf16[800,1600]{1,0:T(8,128)(2,1)} %bitcast.11, bf16[400,800]{1,0:T(8,128)(2,1)} %bitcast.13, bf16[24,400]{1,0:T(8,128)(2,1)} %bitcast.17, ...), custom_call_target="tpu_custom_call" | custom-call | tf_op jit(solution)/shard_map/networks/pallas_call | solution.py:204
  57.6 19.5 %all_to_all.20.r_1_ = f32[32,24,128]{2,1,0:T(8,128)} all-to-all(f32[32,24,128]{2,1,0:T(8,128)} %networks.1), channel_id=1, replica_groups=mesh['z'=8,'core'=2,'member'=16] {'z'}, dimensions={0} | all-to-all | bytes 786432 | tf_op jit(solution)/shard_map/all_to_all | solution.py:209
  77.2 1.8 %pick.1 = f32[32,24,128]{2,1,0:T(8,128)} custom-call(s32[1,128]{1,0:T(1,128)} %table.1.r_0_, f32[32,24,128]{2,1,0:T(8,128)} %all_to_all.20.r_1_), custom_call_target="tpu_custom_call" | custom-call | tf_op jit(solution)/shard_map/pick/pallas_call | solution.py:214
  79.0 7.6 %all-to-all-start.3 = ((f32[32,24,128]{2,1,0:T(8,128)}), f32[32,24,128]{2,1,0:T(8,128)S(1)}, u32[]{:S(2)}, u32[]{:S(2)}) async-start(f32[32,24,128]{2,1,0:T(8,128)} %pick.1), calls=%async_computation.3 | async-start | bytes 786432 | tf_op jit(solution)/shard_map/all_to_all | solution.py:217
  86.6 0.0 copy-done.6
  86.6 1.4 %collective-permute-start.6 = (bf16[1,1536]{1,0:T(2,128)(2,1)S(1)}, bf16[1,1536]{1,0:T(2,128)(2,1)S(1)}, u32[]{:S(2)}, u32[]{:S(2)}) collective-permute-start(bf16[1,1536]{1,0:T(2,128)(2,1)S(1)} %get-tuple-element.10), channel_id=1, source_target_pairs={{0,1},{1,2},{2,3},{3,4},{4,5},{5,6},{6,7},{7,8},{8,9},{9,10},{10,1... | collective-permute-start | bytes 9224 | tf_op jit(solution)/shard_map/ppermute | solution.py:201
  88.0 3.5 %collective-permute-start.7 = (bf16[1,1536]{1,0:T(2,128)(2,1)S(1)}, bf16[1,1536]{1,0:T(2,128)(2,1)S(1)}, u32[]{:S(2)}, u32[]{:S(2)}) collective-permute-start(bf16[1,1536]{1,0:T(2,128)(2,1)S(1)} %get-tuple-element.11), channel_id=1, source_target_pairs={{1,0},{2,1},{3,2},{4,3},{5,4},{6,5},{7,6},{8,7},{9,8},{10,9},{11,1... | collective-permute-start | bytes 9224 | tf_op jit(solution)/shard_map/ppermute | solution.py:202
  91.6 0.0 copy-done.10
  91.6 0.9 collective-permute-start.4
  92.4 0.0 copy-done.9
  92.5 0.0 collective-permute-start.5
  92.5 3.3 %collective-permute-done.6 = bf16[1,1536]{1,0:T(2,128)(2,1)S(1)} collective-permute-done((bf16[1,1536]{1,0:T(2,128)(2,1)S(1)}, bf16[1,1536]{1,0:T(2,128)(2,1)S(1)}, u32[]{:S(2)}, u32[]{:S(2)}) %collective-permute-start.6) | collective-permute-done | bytes 3104 | tf_op jit(solution)/shard_map/ppermute | solution.py:201
  95.7 0.0 collective-permute-done.7
  95.7 0.6 pad_maximum_fusion.y_edges
  96.3 0.0 collective-permute-done.4.up
  96.3 0.0 copy-start.7
  96.3 0.0 collective-permute-done.5.down
  96.4 0.6 copy-done.7
  96.9 0.0 copy-start.8
  96.9 0.6 copy-done.8
  97.5 3.1 %base.1 = f32[24,64,128]{2,1,0:T(8,128)} custom-call(f32[24]{0:T(128)} %diff.1, f32[24,64,128]{2,1,0:T(8,128)} %start.1, f32[24,64,128]{2,1,0:T(8,128)} %state.3, f32[2,64,128]{2,1,0:T(8,128)} %velocity.1, bf16[24,128]{1,0:T(8,128)(2,1)} %copy-done.7, bf16[24,128]{1,0:T(8,128)(2,1)} %copy-done.8, bf16[2,1536]{1,0:T(2,128)(2,1)} %pad_maximum_fusion.y_edges), custom_call_target="tpu_custom_call" | custom-call | tf_op jit(solution)/shard_map/base/pallas_call | solution.py:210
  100.6 0.0 all-to-all-done.3.parts
  100.6 0.0 copy-start.1
  100.7 0.8 copy-done.1
  101.4 3.1 %final.1 = (f32[24,64,128]{2,1,0:T(8,128)}, f32[24,64,128]{2,1,0:T(8,128)}) custom-call(s32[1,128]{1,0:T(1,128)} %table.1.r_0_, s32[1,128]{1,0:T(1,128)} %cells.3, f32[32,24,128]{2,1,0:T(8,128)} %copy-done.1, f32[24,64,128]{2,1,0:T(8,128)} %base.1), custom_call_target="tpu_custom_call" | custom-call | tf_op jit(solution)/shard_map/final/pallas_call | solution.py:218
  (1 shorter events, 0.0 us)
Async XLA Ops:
  0.6 39.2 %collective-permute-start.1 = (bf16[800,1600]{1,0:T(8,128)(2,1)}, bf16[800,1600]{1,0:T(8,128)(2,1)S(1)}, u32[]{:S(2)}, u32[]{:S(2)}) collective-permute-start(bf16[800,1600]{1,0:T(8,128)(2,1)} %bitcast.10), channel_id=1, source_target_pairs={{0,16},{16,0},{1,17},{17,1},{2,18},{18,2},{3,19},{19,3},{4,20},{20... | collective-permute-start | bytes 7680008 | tf_op jit(solution)/shard_map/ppermute | solution.py:184
  3.9 35.9 %collective-permute-start.2 = (bf16[400,800]{1,0:T(8,128)(2,1)}, bf16[400,800]{1,0:T(8,128)(2,1)}, u32[]{:S(2)}, u32[]{:S(2)}) collective-permute-start(bf16[400,800]{1,0:T(8,128)(2,1)} %bitcast.12), channel_id=1, source_target_pairs={{0,16},{16,0},{1,17},{17,1},{2,18},{18,2},{3,19},{19,3},{4,20},{20... | collective-permute-start | bytes 1920008 | tf_op jit(solution)/shard_map/ppermute | solution.py:184
  6.2 14.0 %all-to-all-start = ((bf16[32,24,128]{2,1,0:T(8,128)(2,1)}), bf16[32,24,128]{2,1,0:T(8,128)(2,1)S(1)}, u32[]{:S(2)}, u32[]{:S(2)}) async-start(bf16[32,24,128]{2,1,0:T(8,128)(2,1)} %get-tuple-element.6), calls=%async_computation | async-start | bytes 393216 | tf_op jit(solution)/shard_map/all_to_all | solution.py:192
  20.2 0.7 copy-start.2
  22.5 17.3 %all-to-all-start.1 = ((bf16[32,24,128]{2,1,0:T(8,128)(2,1)}), bf16[32,24,128]{2,1,0:T(8,128)(2,1)S(1)}, u32[]{:S(2)}, u32[]{:S(2)}) async-start(bf16[32,24,128]{2,1,0:T(8,128)(2,1)} %select.1), calls=%async_computation.1 | async-start | bytes 393216 | tf_op jit(solution)/shard_map/all_to_all | solution.py:197
  30.7 2.3 %collective-permute-start = (bf16[24,1600]{1,0:T(8,128)(2,1)}, bf16[24,1600]{1,0:T(8,128)(2,1)S(1)}, u32[]{:S(2)}, u32[]{:S(2)}) collective-permute-start(bf16[24,1600]{1,0:T(8,128)(2,1)} %bitcast.14), channel_id=1, source_target_pairs={{0,16},{16,0},{1,17},{17,1},{2,18},{18,2},{3,19},{19,3},{4,20},{20... | collective-permute-start | bytes 230408 | tf_op jit(solution)/shard_map/ppermute | solution.py:184
  31.6 55.0 %copy-start.6 = (bf16[2,1536]{1,0:T(2,128)(2,1)S(1)}, bf16[2,1536]{1,0:T(2,128)(2,1)}, u32[]{:S(2)}) copy-start(bf16[2,1536]{1,0:T(2,128)(2,1)} %get-tuple-element.9) | copy-start | bytes 18436
  31.6 59.9 %copy-start.10 = (bf16[24,128]{1,0:T(8,128)(2,1)S(1)}, bf16[24,128]{1,0:T(8,128)(2,1)}, u32[]{:S(2)}) copy-start(bf16[24,128]{1,0:T(8,128)(2,1)} %get-tuple-element.7) | copy-start | bytes 18436
  31.6 60.8 %copy-start.9 = (bf16[24,128]{1,0:T(8,128)(2,1)S(1)}, bf16[24,128]{1,0:T(8,128)(2,1)}, u32[]{:S(2)}) copy-start(bf16[24,128]{1,0:T(8,128)(2,1)} %get-tuple-element.8) | copy-start | bytes 18436
  31.6 1.4 %collective-permute-start.3 = (bf16[24,400]{1,0:T(8,128)(2,1)}, bf16[24,400]{1,0:T(8,128)(2,1)S(1)}, u32[]{:S(2)}, u32[]{:S(2)}) collective-permute-start(bf16[24,400]{1,0:T(8,128)(2,1)} %bitcast.16), channel_id=1, source_target_pairs={{0,16},{16,0},{1,17},{17,1},{2,18},{18,2},{3,19},{19,3},{4,20},{20... | collective-permute-start | bytes 57608 | tf_op jit(solution)/shard_map/ppermute | solution.py:184
  33.0 6.8 %copy-start.5 = (bf16[24,400]{1,0:T(8,128)(2,1)}, bf16[24,400]{1,0:T(8,128)(2,1)S(1)}, u32[]{:S(2)}) copy-start(bf16[24,400]{1,0:T(8,128)(2,1)S(1)} %collective-permute-done.3.refs_7_) | copy-start | bytes 57604
  33.0 6.8 %copy-start.4 = (bf16[24,1600]{1,0:T(8,128)(2,1)}, bf16[24,1600]{1,0:T(8,128)(2,1)S(1)}, u32[]{:S(2)}) copy-start(bf16[24,1600]{1,0:T(8,128)(2,1)S(1)} %collective-permute-done.refs_4_) | copy-start | bytes 230404
  39.8 0.7 copy-start.3
  40.5 1.5 %copy-start = (bf16[800,1600]{1,0:T(8,128)(2,1)}, bf16[800,1600]{1,0:T(8,128)(2,1)S(1)}, u32[]{:S(2)}) copy-start(bf16[800,1600]{1,0:T(8,128)(2,1)S(1)} %collective-permute-done.1.refs_5_) | copy-start | bytes 7680004
  79.0 21.7 %all-to-all-start.3 = ((f32[32,24,128]{2,1,0:T(8,128)}), f32[32,24,128]{2,1,0:T(8,128)S(1)}, u32[]{:S(2)}, u32[]{:S(2)}) async-start(f32[32,24,128]{2,1,0:T(8,128)} %pick.1), calls=%async_computation.3 | async-start | bytes 786432 | tf_op jit(solution)/shard_map/all_to_all | solution.py:217
  86.6 9.1 %collective-permute-start.6 = (bf16[1,1536]{1,0:T(2,128)(2,1)S(1)}, bf16[1,1536]{1,0:T(2,128)(2,1)S(1)}, u32[]{:S(2)}, u32[]{:S(2)}) collective-permute-start(bf16[1,1536]{1,0:T(2,128)(2,1)S(1)} %get-tuple-element.10), channel_id=1, source_target_pairs={{0,1},{1,2},{2,3},{3,4},{4,5},{5,6},{6,7},{7,8},{8,9},{9,10},{10,1... | collective-permute-start | bytes 9224 | tf_op jit(solution)/shard_map/ppermute | solution.py:201
  88.0 7.7 %collective-permute-start.7 = (bf16[1,1536]{1,0:T(2,128)(2,1)S(1)}, bf16[1,1536]{1,0:T(2,128)(2,1)S(1)}, u32[]{:S(2)}, u32[]{:S(2)}) collective-permute-start(bf16[1,1536]{1,0:T(2,128)(2,1)S(1)} %get-tuple-element.11), channel_id=1, source_target_pairs={{1,0},{2,1},{3,2},{4,3},{5,4},{6,5},{7,6},{8,7},{9,8},{10,9},{11,1... | collective-permute-start | bytes 9224 | tf_op jit(solution)/shard_map/ppermute | solution.py:202
  91.6 4.8 %collective-permute-start.4 = (bf16[24,128]{1,0:T(8,128)(2,1)S(1)}, bf16[24,128]{1,0:T(8,128)(2,1)S(1)}, u32[]{:S(2)}, u32[]{:S(2)}) collective-permute-start(bf16[24,128]{1,0:T(8,128)(2,1)S(1)} %copy-done.10), channel_id=1, source_target_pairs={{0,16},{16,32},{32,48},{48,64},{64,80},{80,96},{96,112},{112,128},... | collective-permute-start | bytes 18440 | tf_op jit(solution)/shard_map/ppermute | solution.py:199
  92.5 3.9 %collective-permute-start.5 = (bf16[24,128]{1,0:T(8,128)(2,1)S(1)}, bf16[24,128]{1,0:T(8,128)(2,1)S(1)}, u32[]{:S(2)}, u32[]{:S(2)}) collective-permute-start(bf16[24,128]{1,0:T(8,128)(2,1)S(1)} %copy-done.9), channel_id=1, source_target_pairs={{16,0},{32,16},{48,32},{64,48},{80,64},{96,80},{112,96},{128,112},... | collective-permute-start | bytes 18440 | tf_op jit(solution)/shard_map/ppermute | solution.py:200
  96.3 0.6 copy-start.7
  96.9 0.6 copy-start.8
  100.6 0.8 copy-start.1

commit v2 on v1

v2 whole, which is shorter than its diff:
```python
import jax
import jax.numpy as jnp
from jax import lax
from jax.experimental import pallas as pl
from jax.experimental.pallas import tpu as pltpu
from jax.sharding import Mesh, PartitionSpec as P

BF = jnp.bfloat16
F32 = jnp.float32
I32 = jnp.int32
TIME_STEP = 0.25
VM = pl.BlockSpec(memory_space=pltpu.VMEM)
SM = pl.BlockSpec(memory_space=pltpu.SMEM)

ANY = pl.BlockSpec(memory_space=pl.ANY)

SRC, POS, OWN, SIB, N_OWN, N_SIB = 0, 32, 48, 64, 80, 81


def dot(a, b, dims=((1,), (0,))):
    return lax.dot_general(a, b, (dims, ((), ())), preferred_element_type=F32)


def silu(x):
    return (x * lax.logistic(x)).astype(BF)


def in_hbm(array):
    return pltpu.with_memory_space_constraint(array, pltpu.HBM)


def iota(shape, dim):
    return lax.broadcasted_iota(I32, shape, dim)


def table_kernel(team_ref, out):
    z, c = lax.axis_index("z"), lax.axis_index("core")
    n = team_ref.shape[1]
    across = jnp.broadcast_to(team_ref[...].astype(F32), (n, n))
    down = across.T
    row, lane = iota((n, n), 0), iota((n, n), 1)
    before = (across == down) & (lane < row)
    rank = jnp.sum(jnp.where(before, 1.0, 0.0), axis=1, keepdims=True).astype(I32)
    shape = (n, 128)
    g = down[:, :128].astype(I32)
    rank = jnp.broadcast_to(rank, shape)
    b, s = iota(shape, 0), iota(shape, 1)
    core = (rank + g) & 1
    place = ((g >> 1) * 2 + core) * 2 + (g & 1)
    arrives = (b >> 4) * 2 + (g & 1)
    here = (b >> 4) == 2 * z + c
    own = (core == c) & (g == 2 * z + c)
    sib = (core == c) & (g == 2 * z + 1 - c)
    value = jnp.where((s < POS) & here & (place == s), b & 15, jnp.zeros(shape, I32))
    value = jnp.where((s >= POS) & (s < OWN) & here & ((b & 15) == s - POS), place, value)
    value = jnp.where((s >= OWN) & (s < SIB) & own & ((rank >> 1) == s - OWN), arrives, value)
    value = jnp.where((s >= SIB) & (s < N_OWN) & sib & ((rank >> 1) == s - SIB), arrives, value)
    value = jnp.where((s == N_OWN) & own, 1, value)
    value = jnp.where((s == N_SIB) & sib, 1, value)
    out[...] = jnp.sum(value.astype(F32), axis=0, keepdims=True).astype(I32)


def front_kernel(cells, state, blocks, x_low, x_high, y_edges):
    fields, rows, cols = state.shape
    width = cells.shape[1]
    column = cells[...] & (cols - 1)
    line = cells[...] >> (cols.bit_length() - 1)
    picks = jnp.where(iota((cols, width), 0) == column, 1.0, 0.0).astype(BF)
    flat = state[...].astype(BF).reshape(fields * rows, cols)
    found = dot(flat, picks).reshape(fields, rows, width)
    at_row = (iota((rows, width), 0) == line)[None]
    own = jnp.sum(jnp.where(at_row, found, 0.0), axis=1).astype(BF)
    for k in range(blocks.shape[0]):
        blocks[k] = own
    x_low[...] = state[:, 0, :].astype(BF)
    x_high[...] = state[:, rows - 1, :].astype(BF)
    e, j = iota((16, cols), 0), iota((16, cols), 1)
    ends = jnp.where(((e == 0) & (j == 0)) | ((e == 1) & (j == cols - 1)), 1.0, 0.0).astype(BF)
    y_edges[...] = dot(ends, flat, ((1,), (1,)))[0:2].astype(BF)


def select_kernel(base, table, rows, out):
    for k in range(out.shape[0]):
        out[k] = rows[table[0, base + k]]


def network_kernel(table, x, *refs):
    out, rates, sems, load_sems = refs[8], refs[9], refs[10], refs[11]
    own, partner = refs[12:16], [refs[4], refs[16], refs[6], refs[7]]
    loads = [pltpu.make_async_copy(refs[k], own[k], load_sems.at[k]) for k in range(4)]
    loads.append(pltpu.make_async_copy(refs[5], refs[16], load_sems.at[4]))
    for load in loads:
        load.start()

    def copy_of(g, i, a):
        return pltpu.make_async_copy(rates.at[g, i], out.at[a], sems.at[g, i])

    done = 0
    for weights, first, count in ((own, OWN, N_OWN), (partner, SIB, N_SIB)):
        w_in, w_mid, w_low, w_out = weights
        n = table[0, count]
        for load in loads[:4] if weights is own else loads[4:]:
            load.wait()

        def step(k, _, w_in=w_in, w_mid=w_mid, w_low=w_low, w_out=w_out, first=first, n=n, done=done):
            at = [table[0, first + jnp.minimum(4 * k + i, n - 1)] for i in range(4)]
            states = jnp.concatenate([x[i] for i in at], axis=1)
            one = silu(dot(w_in[...], states, ((0,), (0,))))
            two = silu(dot(w_mid[...], one))
            three = silu(dot(w_low[...], two))
            found = dot(w_out[...], three)
            for i, a in enumerate(at):
                rates[done + k, i] = found[:, i * 128 : (i + 1) * 128]

                @pl.when(4 * k + i < n)
                def _(i=i, a=a):
                    copy_of(done + k, i, a).start()

            return 0

        lax.fori_loop(0, (n + 3) // 4, step, 0)
        done = done + (n + 3) // 4

    done = 0
    for count in (N_OWN, N_SIB):
        n = table[0, count]

        def finish(k, _, n=n, done=done):
            for i in range(4):

                @pl.when(4 * k + i < n)
                def _(i=i):
                    copy_of(done + k, i, 0).wait()

            return 0

        lax.fori_loop(0, (n + 3) // 4, finish, 0)
        done = done + (n + 3) // 4


def base_kernel(diff, start, state, velocity, up, down, y_edges, out):
    fields, rows, cols = state.shape
    e, j = iota((2, cols), 0), iota((2, cols), 1)
    ends = jnp.where(((e == 0) & (j == 0)) | ((e == 1) & (j == cols - 1)), 1.0, 0.0).astype(BF)
    sides = dot(y_edges[...], ends, ((0,), (0,))).reshape(fields, rows, cols)
    row, lane = iota((rows, cols), 0), iota((rows, cols), 1)
    half_x, half_y = 0.5 * velocity[0], 0.5 * velocity[1]
    for f in range(fields):
        u = state[f]
        plus_x = jnp.where(row == rows - 1, down[f : f + 1].astype(F32), pltpu.roll(u, rows - 1, 0))
        minus_x = jnp.where(row == 0, up[f : f + 1].astype(F32), pltpu.roll(u, 1, 0))
        plus_y = jnp.where(lane == cols - 1, sides[f], pltpu.roll(u, cols - 1, 1))
        minus_y = jnp.where(lane == 0, sides[f], pltpu.roll(u, 1, 1))
        flow = diff[f] * (plus_x + minus_x + plus_y + minus_y - 4.0 * u)
        flow = flow - half_x * (plus_x - minus_x) - half_y * (plus_y - minus_y)
        out[f] = 0.75 * start[f] + 0.25 * (u + TIME_STEP * flow)


def final_kernel(cells, parts, base, source, new, source_tile, new_tile, sems):
    fields, rows, cols = base.shape
    width = cells.shape[1]
    rates = parts[0]
    for n in range(1, parts.shape[0]):
        rates = rates + parts[n]
    high = rates.astype(BF).astype(F32)
    low = rates - high
    column = cells[...] & (cols - 1)
    line = cells[...] >> (cols.bit_length() - 1)
    at_row = iota((rows, width), 0) == line
    at_col = jnp.where(iota((cols, width), 0) == column, 1.0, 0.0).astype(BF)
    at_col = jnp.concatenate([at_col, at_col], axis=1)
    some = fields // sems.shape[1]
    copies = []
    for k in range(sems.shape[1]):
        spread = []
        for f in range(k * some, (k + 1) * some):
            left = jnp.where(at_row, high[f : f + 1], 0.0)
            right = jnp.where(at_row, low[f : f + 1], 0.0)
            spread.append(jnp.concatenate([left, right], axis=1).astype(BF))
        placed = dot(jnp.concatenate(spread, axis=0), at_col, ((1,), (1,)))
        placed = placed.reshape(some, rows, cols)
        part = pl.ds(k * some, some)
        source_tile[part] = placed
        new_tile[part] = base[part] + (0.25 * TIME_STEP) * placed
        for i, (tile, out) in enumerate(((source_tile, source), (new_tile, new))):
            copies.append(pltpu.make_async_copy(tile.at[part], out.at[part], sems.at[i, k]))
            copies[-1].start()
    for copy in copies:
        copy.wait()


def call(body, out_shape, in_specs, out_specs=None, scratch=(), name=None, mib=8):
    if out_specs is None:
        out_specs = jax.tree.map(lambda _: VM, out_shape)
    return pl.pallas_call(
        body, out_shape=out_shape, in_specs=in_specs, out_specs=out_specs,
        scratch_shapes=scratch, compiler_params=pltpu.CompilerParams(vmem_limit_bytes=mib * 2**20), name=name,
    )


def shards(start, state, velocity, diffusivity, cells, block_team, w_in, w_mid, w_low, w_out):
    fields, rows, cols = state.shape
    width = cells.shape[1]
    sds = jax.ShapeDtypeStruct
    members = lax.axis_size("member")
    teams = lax.axis_size("z") * lax.axis_size("core")
    up = [(i, (i + 1) % 16) for i in range(16)]
    back = [(b, a) for a, b in up]
    swap = [(0, 1), (1, 0)]
    line = ("z", "core")

    weights = [w_in[0, 0].T, w_mid[0, 0], w_low[0, 0], w_out[0, 0]]
    partner = [lax.ppermute(w, "core", swap) for w in weights]

    blocks, x_low, x_high, y_edges = call(
        front_kernel,
        (sds((members, fields, width), BF), sds((fields, cols), BF), sds((fields, cols), BF),
         sds((2, fields * rows), BF)),
        [VM, VM], name="front",
    )(cells, state)
    gathered = lax.all_to_all(blocks, "member", 0, 0, tiled=True)
    table = call(table_kernel, sds((1, 128), I32), [VM], name="table")(block_team.T)
    outgoing = call(
        lambda *r: select_kernel(SRC, *r), sds((2 * teams, fields, width), BF), [SM, VM], name="select"
    )(table, gathered)
    incoming = lax.all_to_all(outgoing, line, 0, 0, tiled=True)

    from_up = lax.ppermute(x_high, line, up)
    from_down = lax.ppermute(x_low, line, back)
    from_left = lax.ppermute(y_edges[1:2], "member", up)
    from_right = lax.ppermute(y_edges[0:1], "member", back)
    incoming, from_up, from_down, from_left, from_right = lax.optimization_barrier(
        (incoming, from_up, from_down, from_left, from_right)
    )

    produced = call(
        network_kernel, sds((2 * teams, fields, width), F32), [SM, VM] + [ANY] * 4 + [VM, ANY, VM, VM], ANY,
        scratch=[pltpu.VMEM((8, 4, fields, width), F32), pltpu.SemaphoreType.DMA((8, 4)), pltpu.SemaphoreType.DMA((5,))]
        + [pltpu.VMEM(w.shape, BF) for w in (*weights, weights[1])],
        name="networks", mib=24,
    )(table, incoming, *[in_hbm(w) for w in weights], partner[0], in_hbm(partner[1]), *partner[2:])
    returned = lax.all_to_all(produced, line, 0, 0, tiled=True)
    base = call(
        base_kernel, sds(state.shape, F32), [SM] + [VM] * 6, name="base"
    )(diffusivity, start, state, velocity, from_up, from_down,
      jnp.concatenate([from_left, from_right], axis=0))
    returned, base = lax.optimization_barrier((returned, base))
    terms = call(
        lambda *r: select_kernel(POS, *r), sds((members, fields, width), F32), [SM, VM], name="pick"
    )(table, returned)
    parts = lax.all_to_all(terms, "member", 0, 0, tiled=True)
    return call(
        final_kernel, (sds(state.shape, F32), sds(state.shape, F32)), [VM, VM, VM], (ANY, ANY),
        scratch=[pltpu.VMEM(state.shape, F32), pltpu.VMEM(state.shape, F32), pltpu.SemaphoreType.DMA((2, 3))],
        name="final",
    )(cells, parts, base)


def solution(mesh):
    team, member = mesh.devices.shape
    own_mesh = Mesh(mesh.devices.reshape(team // 2, 2, member), ("z", "core", "member"))
    line = ("z", "core")
    tile = P(None, line, "member")
    weight = P(line, "member", None, None)
    return jax.shard_map(
        shards,
        mesh=own_mesh,
        in_specs=(tile, tile, tile, P(), P((*line, "member"), None), P(), weight, weight, weight, weight),
        out_specs=(tile, tile),
        check_vma=False,
    )
```

time: 105 us -> 100 us (0.952); the launches traced: 104 us -> 102 us
  waiting for transfers between devices: 17.3 us -> 28.5 us
  Pallas kernels: 29 us -> 20 us
  blocking collectives: 19.5 us -> 12.2 us
  starting transfers between devices: 31.8 us -> 37.8 us
  local copies, waits for them, and re-layouts: 4.83 us -> 2.5 us
  other arithmetic: 1.28 us -> 0.02 us
    all_to_all x1, blocking collectives: 19.5 us -> 12.2 us  [shards(): parts = lax.all_to_all(terms, 'member', 0, 0, tiled=True)]
    pallas_call x6, Pallas kernels: 25.9 us -> 18.7 us  [the longest x1 14.1 us: shards(): call(network_kernel, sds((2 * teams, fields, width), F32), [SM, VM] + [AN...]
    all_to_all x3, starting transfers between devices: 21.6 us -> 27.6 us  [the longest x1 12.2 us: shards(): returned = lax.all_to_all(produced, line, 0, 0, tiled=True)]
    all_to_all x3, waiting for transfers between devices: 12.7 us -> 17.8 us  [the longest x1 13.1 us: shards(): returned = lax.all_to_all(produced, line, 0, 0, tiled=True)]
    ppermute x1, starting transfers between devices: 3.51 us -> 0.01 us  [shards(): from_right = lax.ppermute(y_edges[0:1], 'member', back)]
    ppermute x1, waiting for transfers between devices: 0.01 us -> 2.77 us  [shards(): from_right = lax.ppermute(y_edges[0:1], 'member', back)]
    ppermute x1, starting transfers between devices: 0.9 us -> 3.64 us  [shards(): from_up = lax.ppermute(x_high, line, up)]
    unnamed x22 -> x16, local copies, waits for them, and re-layouts: 4.81 us -> 2.49 us
  transfers between devices with their start and end apart: 11 -> 11, of which waited for: 4 -> 6; matrix products, arithmetic and copies ran while one was open for 1% -> 0% of each run, Pallas kernels for 8% -> 4%
where the time goes in v2:
time: 100 us; the launch traced here: 102 us
  starting transfers between devices  37.8 us (38%)
  waiting for transfers between devices  28.5 us (28%)
  Pallas kernels  20 us (20%)
  blocking collectives  12.2 us (12%)
  local copies, waits for them, and re-layouts  2.5 us (2%)
    pallas_call x1, Pallas kernels, shards(): call(network_kernel, sds((2 * teams, fields, width), F32), [SM, VM] + [AN...  14.1 us
    all_to_all x1, waiting for transfers between devices, shards(): returned = lax.all_to_all(produced, line, 0, 0, tiled=True)  13.1 us
    all_to_all x1, blocking collectives, shards(): parts = lax.all_to_all(terms, 'member', 0, 0, tiled=True)  12.2 us
    all_to_all x1, starting transfers between devices, shards(): returned = lax.all_to_all(produced, line, 0, 0, tiled=True)  12.2 us
    all_to_all x1, starting transfers between devices, shards(): incoming = lax.all_to_all(outgoing, line, 0, 0, tiled=True)  10.3 us
    ppermute x1, waiting for transfers between devices, shards(): from_left = lax.ppermute(y_edges[1:2], 'member', up)  5.55 us
    all_to_all x1, starting transfers between devices, shards(): gathered = lax.all_to_all(blocks, 'member', 0, 0, tiled=True)  5.05 us
    all_to_all x1, waiting for transfers between devices, shards(): gathered = lax.all_to_all(blocks, 'member', 0, 0, tiled=True)  4.7 us
  transfers between devices with their start and end apart: 11, of which 6 were waited for; matrix products, arithmetic and copies ran while one was open for 0% of the time, Pallas kernels for 4%

profile of v2, /device:TPU:1, one launch (start us, length us, event | category | flops | bytes accessed | tf_op | source)
XLA Modules:
  0.0 101.8 jit_solution(3847600634237421093)
XLA Ops:
  0.6 3.3 %collective-permute-start.5 = (bf16[800,1600]{1,0:T(8,128)(2,1)}, bf16[800,1600]{1,0:T(8,128)(2,1)}, u32[]{:S(2)}, u32[]{:S(2)}) collective-permute-start(bf16[800,1600]{1,0:T(8,128)(2,1)} %bitcast.8), channel_id=1, source_target_pairs={{0,16},{16,0},{1,17},{17,1},{2,18},{18,2},{3,19},{19,3},{4,20},{20... | collective-permute-start | bytes 7680008 | tf_op jit(solution)/shard_map/ppermute | solution.py:213
  3.9 0.1 collective-permute-start.6
  4.0 0.0 copy-start
  4.0 1.1 %copy-done = f32[24,64,128]{2,1,0:T(8,128)S(1)} copy-done((f32[24,64,128]{2,1,0:T(8,128)S(1)}, f32[24,64,128]{2,1,0:T(8,128)}, u32[]{:S(2)}) %copy-start) | copy-done | bytes 786456
  5.2 0.0 copy-start.4
  5.2 0.7 copy-done.4
  5.8 1.0 front.1
  6.8 5.0 %all-to-all-start = ((bf16[16,24,128]{2,1,0:T(8,128)(2,1)}), bf16[16,24,128]{2,1,0:T(8,128)(2,1)S(1)}, u32[]{:S(2)}, u32[]{:S(2)}) async-start(bf16[16,24,128]{2,1,0:T(8,128)(2,1)} %get-tuple-element.13), calls=%async_computation | async-start | bytes 196608 | tf_op jit(solution)/shard_map/all_to_all | solution.py:221
  11.9 0.8 collective-permute-start.4
  12.6 0.1 collective-permute-start.7
  12.7 0.0 copy-start.7
  12.7 0.7 copy-done.7
  13.4 0.3 table.1.r_0_
  13.8 4.7 %all-to-all-done.r_1_ = bf16[16,24,128]{2,1,0:T(8,128)(2,1)S(1)} async-done(((bf16[16,24,128]{2,1,0:T(8,128)(2,1)}), bf16[16,24,128]{2,1,0:T(8,128)(2,1)S(1)}, u32[]{:S(2)}, u32[]{:S(2)}) %all-to-all-start) | async-done | bytes 98336 | tf_op jit(solution)/shard_map/all_to_all | solution.py:221
  18.5 1.2 %select.1 = bf16[32,24,128]{2,1,0:T(8,128)(2,1)} custom-call(s32[1,128]{1,0:T(1,128)S(1)} %table.1.r_0_, bf16[16,24,128]{2,1,0:T(8,128)(2,1)S(1)} %all-to-all-done.r_1_), custom_call_target="tpu_custom_call" | custom-call | tf_op jit(solution)/shard_map/select/pallas_call | solution.py:223
  19.7 10.3 %all-to-all-start.1 = ((bf16[32,24,128]{2,1,0:T(8,128)(2,1)}), bf16[32,24,128]{2,1,0:T(8,128)(2,1)S(1)}, u32[]{:S(2)}, u32[]{:S(2)}) async-start(bf16[32,24,128]{2,1,0:T(8,128)(2,1)} %select.1), calls=%async_computation.1 | async-start | bytes 393216 | tf_op jit(solution)/shard_map/all_to_all | solution.py:226
  30.0 0.3 collective-permute-start.2
  30.4 5.6 %collective-permute-done.2 = bf16[1,1536]{1,0:T(2,128)(2,1)S(1)} collective-permute-done((bf16[1,1536]{1,0:T(2,128)(2,1)S(1)}, bf16[1,1536]{1,0:T(2,128)(2,1)S(1)}, u32[]{:S(2)}, u32[]{:S(2)}) %collective-permute-start.2) | collective-permute-done | bytes 3104 | tf_op jit(solution)/shard_map/ppermute | solution.py:230
  35.9 0.0 collective-permute-start.3
  35.9 2.8 %collective-permute-done.3 = bf16[1,1536]{1,0:T(2,128)(2,1)S(1)} collective-permute-done((bf16[1,1536]{1,0:T(2,128)(2,1)S(1)}, bf16[1,1536]{1,0:T(2,128)(2,1)S(1)}, u32[]{:S(2)}, u32[]{:S(2)}) %collective-permute-start.3) | collective-permute-done | bytes 3104 | tf_op jit(solution)/shard_map/ppermute | solution.py:231
  38.7 3.6 %collective-permute-start = (bf16[24,128]{1,0:T(8,128)(2,1)S(1)}, bf16[24,128]{1,0:T(8,128)(2,1)S(1)}, u32[]{:S(2)}, u32[]{:S(2)}) collective-permute-start(bf16[24,128]{1,0:T(8,128)(2,1)S(1)} %get-tuple-element.14), channel_id=1, source_target_pairs={{0,16},{16,32},{32,48},{48,64},{64,80},{80,96},{96,112},{112,128},... | collective-permute-start | bytes 18440 | tf_op jit(solution)/shard_map/ppermute | solution.py:228
  42.3 0.8 collective-permute-done.up
  43.1 0.0 copy-start.1
  43.1 0.0 copy-start.2
  43.1 0.0 copy-start.3
  43.1 0.0 copy-start.6
  43.1 2.0 %collective-permute-start.1 = (bf16[24,128]{1,0:T(8,128)(2,1)S(1)}, bf16[24,128]{1,0:T(8,128)(2,1)S(1)}, u32[]{:S(2)}, u32[]{:S(2)}) collective-permute-start(bf16[24,128]{1,0:T(8,128)(2,1)S(1)} %get-tuple-element.15), channel_id=1, source_target_pairs={{16,0},{32,16},{48,32},{64,48},{80,64},{96,80},{112,96},{128,112},... | collective-permute-start | bytes 18440 | tf_op jit(solution)/shard_map/ppermute | solution.py:229
  45.1 1.6 %collective-permute-done.1.down = bf16[24,128]{1,0:T(8,128)(2,1)S(1)} collective-permute-done((bf16[24,128]{1,0:T(8,128)(2,1)S(1)}, bf16[24,128]{1,0:T(8,128)(2,1)S(1)}, u32[]{:S(2)}, u32[]{:S(2)}) %collective-permute-start.1) | collective-permute-done | bytes 6176 | tf_op jit(solution)/shard_map/ppermute | solution.py:229
  46.7 0.0 all-to-all-done.1.x
  46.7 0.0 collective-permute-done.7.refs_7_
  46.7 0.0 collective-permute-done.4.refs_4_
  46.7 0.0 collective-permute-done.6.refs_6_
  46.7 0.0 collective-permute-done.5.refs_5_
  46.8 14.1 %networks.1 = f32[32,24,128]{2,1,0:T(8,128)} custom-call(s32[1,128]{1,0:T(1,128)S(1)} %table.1.r_0_, bf16[32,24,128]{2,1,0:T(8,128)(2,1)S(1)} %all-to-all-done.1.x, bf16[24,1600]{1,0:T(8,128)(2,1)} %bitcast.13, bf16[800,1600]{1,0:T(8,128)(2,1)} %bitcast.9, bf16[400,800]{1,0:T(8,128)(2,1)} %bitcast.11, bf16[24,400]{1,0:T(8,128)(2,1)} %bitcast.15, ...), custom_call_target="tpu_custom_call" | custom-call | tf_op jit(solution)/shard_map/networks/pallas_call | solution.py:236
  60.9 0.0 copy-start.5
  60.9 12.2 %all-to-all-start.2 = ((f32[32,24,128]{2,1,0:T(8,128)}), f32[32,24,128]{2,1,0:T(8,128)S(1)}, u32[]{:S(2)}, u32[]{:S(2)}) async-start(f32[32,24,128]{2,1,0:T(8,128)} %networks.1), calls=%async_computation.2 | async-start | bytes 786432 | tf_op jit(solution)/shard_map/all_to_all | solution.py:242
  73.1 0.0 copy-done.1
  73.1 0.0 copy-done.2
  73.1 0.0 copy-done.3
  73.1 0.0 copy-done.6
  73.1 1.4 %base.1 = f32[24,64,128]{2,1,0:T(8,128)S(1)} custom-call(f32[24]{0:T(128)S(1)} %copy-done.6, f32[24,64,128]{2,1,0:T(8,128)S(1)} %copy-done.2, f32[24,64,128]{2,1,0:T(8,128)S(1)} %copy-done.1, f32[2,64,128]{2,1,0:T(8,128)S(1)} %copy-done.3, bf16[24,128]{1,0:T(8,128)(2,1)S(1)} %collective-permute-done.up, bf16[24,128]{1,0:T(8,128)(2,1)S(1)} %collective-permute-done.1.down, ...), custom_call_target="tpu_custom_call" | custom-call | tf_op jit(solution)/shard_map/base/pallas_call | solution.py:243
  74.5 13.1 %all-to-all-done.2.r_1_ = f32[32,24,128]{2,1,0:T(8,128)S(1)} async-done(((f32[32,24,128]{2,1,0:T(8,128)}), f32[32,24,128]{2,1,0:T(8,128)S(1)}, u32[]{:S(2)}, u32[]{:S(2)}) %all-to-all-start.2) | async-done | bytes 393248 | tf_op jit(solution)/shard_map/all_to_all | solution.py:242
  87.6 0.6 pick.1
  88.1 12.2 %all_to_all.20.parts = f32[16,24,128]{2,1,0:T(8,128)S(1)} all-to-all(f32[16,24,128]{2,1,0:T(8,128)S(1)} %pick.1), channel_id=1, replica_groups=mesh['z'=8,'core'=2,'member'=16] {'member'}, dimensions={0} | all-to-all | bytes 393216 | tf_op jit(solution)/shard_map/all_to_all | solution.py:251
  100.3 0.0 copy-done.5
  100.3 1.4 %final.1 = (f32[24,64,128]{2,1,0:T(8,128)}, f32[24,64,128]{2,1,0:T(8,128)}) custom-call(s32[1,128]{1,0:T(1,128)S(1)} %copy-done.5, f32[16,24,128]{2,1,0:T(8,128)S(1)} %all_to_all.20.parts, f32[24,64,128]{2,1,0:T(8,128)S(1)} %base.1), custom_call_target="tpu_custom_call" | custom-call | tf_op jit(solution)/shard_map/final/pallas_call | solution.py:252
  (2 shorter events, 0.0 us)
Async XLA Ops:
  0.6 46.1 %collective-permute-start.5 = (bf16[800,1600]{1,0:T(8,128)(2,1)}, bf16[800,1600]{1,0:T(8,128)(2,1)}, u32[]{:S(2)}, u32[]{:S(2)}) collective-permute-start(bf16[800,1600]{1,0:T(8,128)(2,1)} %bitcast.8), channel_id=1, source_target_pairs={{0,16},{16,0},{1,17},{17,1},{2,18},{18,2},{3,19},{19,3},{4,20},{20... | collective-permute-start | bytes 7680008 | tf_op jit(solution)/shard_map/ppermute | solution.py:213
  3.9 42.8 %collective-permute-start.6 = (bf16[400,800]{1,0:T(8,128)(2,1)}, bf16[400,800]{1,0:T(8,128)(2,1)S(1)}, u32[]{:S(2)}, u32[]{:S(2)}) collective-permute-start(bf16[400,800]{1,0:T(8,128)(2,1)} %bitcast.10), channel_id=1, source_target_pairs={{0,16},{16,0},{1,17},{17,1},{2,18},{18,2},{3,19},{19,3},{4,20},{20... | collective-permute-start | bytes 1920008 | tf_op jit(solution)/shard_map/ppermute | solution.py:213
  4.0 1.1 %copy-start = (f32[24,64,128]{2,1,0:T(8,128)S(1)}, f32[24,64,128]{2,1,0:T(8,128)}, u32[]{:S(2)}) copy-start(f32[24,64,128]{2,1,0:T(8,128)} %state.3) | copy-start | bytes 2359300
  5.2 0.7 copy-start.4
  6.8 11.7 %all-to-all-start = ((bf16[16,24,128]{2,1,0:T(8,128)(2,1)}), bf16[16,24,128]{2,1,0:T(8,128)(2,1)S(1)}, u32[]{:S(2)}, u32[]{:S(2)}) async-start(bf16[16,24,128]{2,1,0:T(8,128)(2,1)} %get-tuple-element.13), calls=%async_computation | async-start | bytes 196608 | tf_op jit(solution)/shard_map/all_to_all | solution.py:221
  11.9 34.9 %collective-permute-start.4 = (bf16[24,1600]{1,0:T(8,128)(2,1)}, bf16[24,1600]{1,0:T(8,128)(2,1)S(1)}, u32[]{:S(2)}, u32[]{:S(2)}) collective-permute-start(bf16[24,1600]{1,0:T(8,128)(2,1)} %bitcast.12), channel_id=1, source_target_pairs={{0,16},{16,0},{1,17},{17,1},{2,18},{18,2},{3,19},{19,3},{4,20},{20... | collective-permute-start | bytes 230408 | tf_op jit(solution)/shard_map/ppermute | solution.py:213
  12.6 34.1 %collective-permute-start.7 = (bf16[24,400]{1,0:T(8,128)(2,1)}, bf16[24,400]{1,0:T(8,128)(2,1)S(1)}, u32[]{:S(2)}, u32[]{:S(2)}) collective-permute-start(bf16[24,400]{1,0:T(8,128)(2,1)} %bitcast.14), channel_id=1, source_target_pairs={{0,16},{16,0},{1,17},{17,1},{2,18},{18,2},{3,19},{19,3},{4,20},{20... | collective-permute-start | bytes 57608 | tf_op jit(solution)/shard_map/ppermute | solution.py:213
  12.7 0.7 copy-start.7
  19.7 27.0 %all-to-all-start.1 = ((bf16[32,24,128]{2,1,0:T(8,128)(2,1)}), bf16[32,24,128]{2,1,0:T(8,128)(2,1)S(1)}, u32[]{:S(2)}, u32[]{:S(2)}) async-start(bf16[32,24,128]{2,1,0:T(8,128)(2,1)} %select.1), calls=%async_computation.1 | async-start | bytes 393216 | tf_op jit(solution)/shard_map/all_to_all | solution.py:226
  30.0 5.9 %collective-permute-start.2 = (bf16[1,1536]{1,0:T(2,128)(2,1)S(1)}, bf16[1,1536]{1,0:T(2,128)(2,1)S(1)}, u32[]{:S(2)}, u32[]{:S(2)}) collective-permute-start(bf16[1,1536]{1,0:T(2,128)(2,1)S(1)} %get-tuple-element.25), channel_id=1, source_target_pairs={{0,1},{1,2},{2,3},{3,4},{4,5},{5,6},{6,7},{7,8},{8,9},{9,10},{10,1... | collective-permute-start | bytes 9224 | tf_op jit(solution)/shard_map/ppermute | solution.py:230
  35.9 2.8 %collective-permute-start.3 = (bf16[1,1536]{1,0:T(2,128)(2,1)S(1)}, bf16[1,1536]{1,0:T(2,128)(2,1)S(1)}, u32[]{:S(2)}, u32[]{:S(2)}) collective-permute-start(bf16[1,1536]{1,0:T(2,128)(2,1)S(1)} %get-tuple-element.24), channel_id=1, source_target_pairs={{1,0},{2,1},{3,2},{4,3},{5,4},{6,5},{7,6},{8,7},{9,8},{10,9},{11,1... | collective-permute-start | bytes 9224 | tf_op jit(solution)/shard_map/ppermute | solution.py:231
  38.7 4.4 %collective-permute-start = (bf16[24,128]{1,0:T(8,128)(2,1)S(1)}, bf16[24,128]{1,0:T(8,128)(2,1)S(1)}, u32[]{:S(2)}, u32[]{:S(2)}) collective-permute-start(bf16[24,128]{1,0:T(8,128)(2,1)S(1)} %get-tuple-element.14), channel_id=1, source_target_pairs={{0,16},{16,32},{32,48},{48,64},{64,80},{80,96},{96,112},{112,128},... | collective-permute-start | bytes 18440 | tf_op jit(solution)/shard_map/ppermute | solution.py:228
  43.1 30.0 %copy-start.1 = (f32[24,64,128]{2,1,0:T(8,128)S(1)}, f32[24,64,128]{2,1,0:T(8,128)}, u32[]{:S(2)}) copy-start(f32[24,64,128]{2,1,0:T(8,128)} %state.3) | copy-start | bytes 2359300
  43.1 30.0 %copy-start.2 = (f32[24,64,128]{2,1,0:T(8,128)S(1)}, f32[24,64,128]{2,1,0:T(8,128)}, u32[]{:S(2)}) copy-start(f32[24,64,128]{2,1,0:T(8,128)} %start.1) | copy-start | bytes 2359300
  43.1 30.0 %copy-start.3 = (f32[2,64,128]{2,1,0:T(8,128)S(1)}, f32[2,64,128]{2,1,0:T(8,128)}, u32[]{:S(2)}) copy-start(f32[2,64,128]{2,1,0:T(8,128)} %velocity.1) | copy-start | bytes 196612
  43.1 30.0 %copy-start.6 = (f32[24]{0:T(128)S(1)}, f32[24]{0:T(128)}, u32[]{:S(2)}) copy-start(f32[24]{0:T(128)} %diff.1) | copy-start | bytes 292
  43.1 3.6 %collective-permute-start.1 = (bf16[24,128]{1,0:T(8,128)(2,1)S(1)}, bf16[24,128]{1,0:T(8,128)(2,1)S(1)}, u32[]{:S(2)}, u32[]{:S(2)}) collective-permute-start(bf16[24,128]{1,0:T(8,128)(2,1)S(1)} %get-tuple-element.15), channel_id=1, source_target_pairs={{16,0},{32,16},{48,32},{64,48},{80,64},{96,80},{112,96},{128,112},... | collective-permute-start | bytes 18440 | tf_op jit(solution)/shard_map/ppermute | solution.py:229
  60.9 39.5 %copy-start.5 = (s32[1,128]{1,0:T(1,128)S(1)}, s32[1,128]{1,0:T(1,128)}, u32[]{:S(2)}) copy-start(s32[1,128]{1,0:T(1,128)} %cells.3) | copy-start | bytes 1540
  60.9 26.7 %all-to-all-start.2 = ((f32[32,24,128]{2,1,0:T(8,128)}), f32[32,24,128]{2,1,0:T(8,128)S(1)}, u32[]{:S(2)}, u32[]{:S(2)}) async-start(f32[32,24,128]{2,1,0:T(8,128)} %networks.1), calls=%async_computation.2 | async-start | bytes 786432 | tf_op jit(solution)/shard_map/all_to_all | solution.py:242
